TPU v7x, 32 devices: a whole 2x2x4 slice. The times are simulated.
32 devices in a mesh: dp: 4 (over z), tp: 8 (over y, x, core).
Axes of the slice: x: 2, y: 2, z: 4, core: 2. Of those that a mesh axis runs over, the one named last changes fastest.
Arguments:
- x_in: bfloat16 [3, 2, 48, 384, 1024], P(None, None, 'dp')
- u_pre: bfloat16 [3, 2, 48, 384, 4096], P(None, None, 'dp', None, 'tp')
- w_up: bfloat16 [3, 1024, 4096], P(None, None, 'tp')
- w_down: bfloat16 [3, 4096, 1024], P(None, 'tp')
- d_out: bfloat16 [2, 48, 384, 1024], P(None, 'dp')
- noise_up: float32 [3, 1024, 4096], P(None, 'dp', 'tp')
- noise_down: float32 [3, 4096, 1024], P(None, 'tp', 'dp')
- clip_norm: float32 [1], replicated
- noise_mult: float32 [1], replicated
Outputs:
- output 1: float32 [3, 1024, 4096], P(None, 'dp', 'tp')
- output 2: float32 [3, 4096, 1024], P(None, 'tp', 'dp')
- output 3: bfloat16 [2, 48, 384, 1024], P(None, 'dp')
All inputs are finite; a program needn't handle non-finite values.
Results may differ from a plain program's by a relative error of at most 0.0169951.
Values are sent between devices in bfloat16 or wider.
A program may use at most 1 GiB of HBM per device.

v0:
```python
import jax
import jax.numpy as jnp
from jax import lax
from jax.sharding import PartitionSpec as P, NamedSharding


def solution(mesh):
    dp_size = mesh.shape["dp"]

    def local_pass(x_in, u_pre, w_up, w_down, d_out, noise_up, noise_down, clip_norm, noise_mult):
        n_layers = x_in.shape[0]
        examples = d_out.shape[0] * d_out.shape[1] * dp_size
        grad_cot = d_out
        norm_part = jnp.zeros(d_out.shape[:2], jnp.float32)
        saved_acts = []
        for layer_idx in reversed(range(n_layers)):
            x_layer = x_in[layer_idx]
            gelu_out, gelu_vjp = jax.vjp(jax.nn.gelu, u_pre[layer_idx].astype(jnp.float32))
            hidden = gelu_out.astype(jnp.bfloat16)
            d_act = jnp.einsum("mbtd,nd->mbtn", grad_cot, w_down[layer_idx], preferred_element_type=jnp.float32)
            d_hid = gelu_vjp(d_act)[0].astype(jnp.bfloat16)
            part_back = jnp.einsum("mbtn,dn->mbtd", d_hid, w_up[layer_idx], preferred_element_type=jnp.float32).astype(jnp.bfloat16)
            back_sum = lax.psum(part_back, "tp")
            gram_hid = jnp.einsum("mbtn,mbsn->mbts", hidden, hidden, preferred_element_type=jnp.float32)
            gram_cot = jnp.einsum("mbtd,mbsd->mbts", grad_cot, grad_cot, preferred_element_type=jnp.float32)
            gram_x = jnp.einsum("mbtd,mbsd->mbts", x_layer, x_layer, preferred_element_type=jnp.float32)
            gram_dh = jnp.einsum("mbtn,mbsn->mbts", d_hid, d_hid, preferred_element_type=jnp.float32)
            norm_part = norm_part + jnp.sum(gram_hid * gram_cot + gram_x * gram_dh, axis=(2, 3))
            saved_acts.append((layer_idx, x_layer, hidden, d_hid, grad_cot))
            grad_cot = (grad_cot.astype(jnp.float32) + back_sum.astype(jnp.float32)).astype(jnp.bfloat16)
        norm_vec = lax.psum(norm_part, "tp")
        clip_col = jnp.minimum(1.0, clip_norm[0] / jnp.sqrt(norm_vec))[:, :, None, None]
        noise_scale = noise_mult[0] * clip_norm[0]
        up_grads = [None] * n_layers
        down_grads = [None] * n_layers
        for layer_idx, x_layer, hidden, d_hid, cot_layer in saved_acts:
            scaled_dh = (d_hid * clip_col).astype(jnp.bfloat16)
            scaled_cot = (cot_layer * clip_col).astype(jnp.bfloat16)
            up_part = jnp.einsum("mbtd,mbtn->dn", x_layer, scaled_dh, preferred_element_type=jnp.float32)
            down_part = jnp.einsum("mbtn,mbtd->nd", hidden, scaled_cot, preferred_element_type=jnp.float32)
            up_sum = lax.psum_scatter(up_part, "dp", scatter_dimension=0, tiled=True)
            down_sum = lax.psum_scatter(down_part, "dp", scatter_dimension=1, tiled=True)
            up_grads[layer_idx] = (up_sum + noise_scale * noise_up[layer_idx]) / examples
            down_grads[layer_idx] = (down_sum + noise_scale * noise_down[layer_idx]) / examples
        return jnp.stack(up_grads), jnp.stack(down_grads), grad_cot

    in_specs = (P(None, None, "dp", None, None), P(None, None, "dp", None, "tp"), P(None, None, "tp"), P(None, "tp", None), P(None, "dp", None, None), P(None, "dp", "tp"), P(None, "tp", "dp"), P(), P())
    out_specs = (P(None, "dp", "tp"), P(None, "tp", "dp"), P(None, "dp", None, None))
    return jax.shard_map(local_pass, mesh=mesh, in_specs=in_specs, out_specs=out_specs, check_vma=False)
```

profile of v0, /device:TPU:0, one launch (start us, length us, event | category | flops | bytes accessed | tf_op | source)
XLA Modules:
  0.0 1183.4 jit_solution(6748162066128887845)
XLA Ops:
  7.2 27.7 %fusion.17 = bf16[2,12,384,512]{3,2,1,0:T(8,128)(2,1)} fusion(bf16[3,2,12,384,512]{4,3,2,1,0:T(8,128)(2,1)} %param.10, bf16[2,12,384,1024]{3,2,1,0:T(8,128)(2,1)} %param.13, bf16[3,512,1024]{2,1,0:T(8,128)(2,1)} %param.12), kind=kOutput, calls=%fused_computation.38 | convolution fusion | flops 9762766848 | bytes 38797312 | tf_op jit(solution)/shard_map/mbtd,nd->mbtn/dot_general | solution.py:20
  34.9 16.7 %convolution_convert_fusion.2 = bf16[2,12,384,1024]{3,2,1,0:T(8,128)(2,1)} fusion(bf16[2,12,384,512]{3,2,1,0:T(8,128)(2,1)} %fusion.17, bf16[3,1024,512]{2,1,0:T(8,128)(2,1)} %param.11), kind=kOutput, calls=%fused_computation.80 | convolution fusion | flops 9673113600 | bytes 29360128 | tf_op jit(solution)/shard_map/mbtn,dn->mbtd/dot_general | solution.py:22
  51.7 25.7 %fusion.29 = (bf16[2,12,384,512]{3,2,1,0:T(8,128)(2,1)}, bf16[2,12,384,512]{3,2,1,0:T(8,128)(2,1)}, bf16[2,12,384,512]{3,2,1,0:T(8,128)(2,1)}) fusion(bf16[3,2,12,384,512]{4,3,2,1,0:T(8,128)(2,1)} %param.10), kind=kLoop, calls=%fused_computation.50 | loop fusion | flops 141557760 | bytes 56623104 | tf_op jit(solution)/shard_map/convert_element_type | solution.py:19
  106.1 21.7 %fusion.119 = f32[2,12,384,384]{3,2,1,0:T(8,128)} fusion(bf16[2,12,384,1024]{3,2,1,0:T(8,128)(2,1)} %param.13), kind=kOutput, calls=%fused_computation.132 | convolution fusion | flops 7247757312 | bytes 33030144 | tf_op jit(solution)/shard_map/mbtd,mbsd->mbts/dot_general | solution.py:25
  127.9 25.0 %fusion.118 = f32[2,12,384,384]{3,2,1,0:T(8,128)} fusion(bf16[2,12,384,512]{3,2,1,0:T(8,128)(2,1)} %get-tuple-element.10), kind=kOutput, calls=%fused_computation.131 | convolution fusion | flops 3623878656 | bytes 23592960 | tf_op jit(solution)/shard_map/mbtn,mbsn->mbts/dot_general | solution.py:24
  152.8 30.2 %add_reduce_fusion.2 = f32[2,12]{1,0:T(2,128)} fusion(f32[2,12,384,384]{3,2,1,0:T(8,128)} %fusion.120, f32[2,12,384,384]{3,2,1,0:T(8,128)} %fusion.118, f32[2,12,384,384]{3,2,1,0:T(8,128)} %fusion.119, bf16[3,2,12,384,1024]{4,3,2,1,0:T(8,128)(2,1)} %param.9), kind=kOutput, calls=%fused_computation.77 | convolution fusion | flops 7261913088 | bytes 61341792 | tf_op jit(solution)/shard_map/mbtd,mbsd->mbts/dot_general | solution.py:26
  183.0 40.1 %slice_bitcast_fusion = (bf16[2,12,384,1024]{3,2,1,0:T(8,128)(2,1)}, bf16[2,12,384,1024]{3,2,1,0:T(8,128)(2,1)}, bf16[2,12,384,1024]{3,2,1,0:T(8,128)(2,1)}) fusion(bf16[3,2,12,384,1024]{4,3,2,1,0:T(8,128)(2,1)} %param.9), kind=kLoop, calls=%fused_computation.72 | loop fusion | bytes 113246208 | tf_op jit(solution)/shard_map/squeeze | solution.py:17
  223.1 70.1 %all-reduce.4.cloned.1.call-done = bf16[2,12,384,1024]{3,2,1,0:T(8,128)(2,1)} async-done(((bf16[2,12,384,1024]{3,2,1,0:T(8,128)(2,1)}), bf16[2,12,384,1024]{3,2,1,0:T(8,128)(2,1)}) %all-reduce.4.cloned.1.call-update) | async-done | bytes 18874384 | tf_op jit(solution)/shard_map/psum | solution.py:23
  293.2 16.6 %fusion = bf16[2,12,384,1024]{3,2,1,0:T(8,128)(2,1)S(1)} fusion(bf16[2,12,384,1024]{3,2,1,0:T(8,128)(2,1)} %param.13, bf16[2,12,384,1024]{3,2,1,0:T(8,128)(2,1)} %all-reduce.4.cloned.1.call-done), kind=kLoop, calls=%fused_computation.6 | loop fusion | flops 37748736 | bytes 56623104 | tf_op jit(solution)/shard_map/convert_element_type | solution.py:30
  316.3 25.3 %fusion.14 = bf16[2,12,384,512]{3,2,1,0:T(8,128)(2,1)} fusion(bf16[3,2,12,384,512]{4,3,2,1,0:T(8,128)(2,1)} %param.10, bf16[2,12,384,1024]{3,2,1,0:T(8,128)(2,1)S(1)} %fusion, bf16[3,512,1024]{2,1,0:T(8,128)(2,1)} %param.12), kind=kOutput, calls=%fused_computation.35 | convolution fusion | flops 9762766848 | bytes 38797312 | tf_op jit(solution)/shard_map/mbtd,nd->mbtn/dot_general | solution.py:20
  341.5 16.5 %convolution_convert_fusion.1 = bf16[2,12,384,1024]{3,2,1,0:T(8,128)(2,1)} fusion(bf16[2,12,384,512]{3,2,1,0:T(8,128)(2,1)} %fusion.14, bf16[3,1024,512]{2,1,0:T(8,128)(2,1)} %param.11), kind=kOutput, calls=%fused_computation.79 | convolution fusion | flops 9673113600 | bytes 29360128 | tf_op jit(solution)/shard_map/mbtn,dn->mbtd/dot_general | solution.py:22
  372.6 21.6 %fusion.122 = f32[2,12,384,384]{3,2,1,0:T(8,128)} fusion(bf16[2,12,384,1024]{3,2,1,0:T(8,128)(2,1)} %copy-done), kind=kOutput, calls=%fused_computation.135 | convolution fusion | flops 7247757312 | bytes 33030144 | tf_op jit(solution)/shard_map/mbtd,mbsd->mbts/dot_general | solution.py:25
  408.5 29.1 %add_reduce_fusion.1 = f32[2,12]{1,0:T(2,128)S(1)} fusion(f32[2,12,384,384]{3,2,1,0:T(8,128)} %fusion.123, f32[2,12,384,384]{3,2,1,0:T(8,128)} %fusion.121, f32[2,12,384,384]{3,2,1,0:T(8,128)} %fusion.122, bf16[3,2,12,384,1024]{4,3,2,1,0:T(8,128)(2,1)} %param.9), kind=kOutput, calls=%fused_computation.76 | convolution fusion | flops 7261913088 | bytes 61341792 | tf_op jit(solution)/shard_map/mbtd,mbsd->mbts/dot_general | solution.py:26
  437.6 159.4 %all-reduce.6.cloned.1.call-done = bf16[2,12,384,1024]{3,2,1,0:T(8,128)(2,1)} async-done(((bf16[2,12,384,1024]{3,2,1,0:T(8,128)(2,1)}), bf16[2,12,384,1024]{3,2,1,0:T(8,128)(2,1)}) %all-reduce.6.cloned.1.call-update) | async-done | bytes 18874384 | tf_op jit(solution)/shard_map/psum | solution.py:23
  596.9 16.6 %fusion.2 = bf16[2,12,384,1024]{3,2,1,0:T(8,128)(2,1)S(1)} fusion(bf16[2,12,384,1024]{3,2,1,0:T(8,128)(2,1)} %copy-done, bf16[2,12,384,1024]{3,2,1,0:T(8,128)(2,1)} %all-reduce.6.cloned.1.call-done), kind=kLoop, calls=%fused_computation.8 | loop fusion | flops 37748736 | bytes 56623104 | tf_op jit(solution)/shard_map/convert_element_type | solution.py:30
  619.8 25.6 %fusion.11 = bf16[2,12,384,512]{3,2,1,0:T(8,128)(2,1)} fusion(bf16[3,2,12,384,512]{4,3,2,1,0:T(8,128)(2,1)} %param.10, bf16[2,12,384,1024]{3,2,1,0:T(8,128)(2,1)S(1)} %fusion.2, bf16[3,512,1024]{2,1,0:T(8,128)(2,1)} %param.12), kind=kOutput, calls=%fused_computation.32 | convolution fusion | flops 9762766848 | bytes 38797312 | tf_op jit(solution)/shard_map/mbtd,nd->mbtn/dot_general | solution.py:20
  645.5 16.5 %convolution_convert_fusion = bf16[2,12,384,1024]{3,2,1,0:T(8,128)(2,1)} fusion(bf16[2,12,384,512]{3,2,1,0:T(8,128)(2,1)} %fusion.11, bf16[3,1024,512]{2,1,0:T(8,128)(2,1)} %param.11), kind=kOutput, calls=%fused_computation.78 | convolution fusion | flops 9673113600 | bytes 29360128 | tf_op jit(solution)/shard_map/mbtn,dn->mbtd/dot_general | solution.py:22
  662.0 21.8 %fusion.125 = f32[2,12,384,384]{3,2,1,0:T(8,128)} fusion(bf16[2,12,384,1024]{3,2,1,0:T(8,128)(2,1)} %copy-done.1), kind=kOutput, calls=%fused_computation.138 | convolution fusion | flops 7247757312 | bytes 33030144 | tf_op jit(solution)/shard_map/mbtd,mbsd->mbts/dot_general | solution.py:25
  698.1 29.1 %add_reduce_fusion = f32[2,12]{1,0:T(2,128)S(1)} fusion(f32[2,12,384,384]{3,2,1,0:T(8,128)} %fusion.126, f32[2,12,384,384]{3,2,1,0:T(8,128)} %fusion.124, f32[2,12,384,384]{3,2,1,0:T(8,128)} %fusion.125, bf16[3,2,12,384,1024]{4,3,2,1,0:T(8,128)(2,1)} %param.9), kind=kOutput, calls=%fused_computation.75 | convolution fusion | flops 7261913088 | bytes 61341792 | tf_op jit(solution)/shard_map/mbtd,mbsd->mbts/dot_general | solution.py:26
  741.0 19.2 %multiply_convert_fusion.2 = (bf16[2,12,384,512]{3,2,1,0:T(8,128)(2,1)}, bf16[2,12,384,512]{3,2,1,0:T(8,128)(2,1)}, bf16[2,12,384,512]{3,2,1,0:T(8,128)(2,1)}) fusion(bf16[2,12,384,512]{3,2,1,0:T(8,128)(2,1)} %fusion.11, f32[2,12]{1,0:T(2,128)S(1)} %multiply_minimum_fusion, bf16[2,12,384,512]{3,2,1,0:T(8,128)(2,1)} %fusion.14, ...), kind=kLoop, calls=%fused_computation.71 | loop fusion | flops 42467328 | bytes 56623200 | tf_op jit(solution)/shard_map/convert_element_type | solution.py:37
  760.2 17.6 %fusion.54 = f32[1024,512]{0,1:T(8,128)} fusion(bf16[2,12,384,1024]{3,2,1,0:T(8,128)(2,1)} %get-tuple-element.6, bf16[2,12,384,512]{3,2,1,0:T(8,128)(2,1)} %get-tuple-element.22), kind=kOutput, calls=%fused_computation.87 | convolution fusion | flops 9663676416 | bytes 30408704 | tf_op jit(solution)/shard_map/mbtd,mbtn->dn/dot_general | solution.py:39
  777.9 17.7 %fusion.59 = f32[1024,512]{0,1:T(8,128)} fusion(bf16[2,12,384,1024]{3,2,1,0:T(8,128)(2,1)} %get-tuple-element.8, bf16[2,12,384,512]{3,2,1,0:T(8,128)(2,1)} %get-tuple-element.23), kind=kOutput, calls=%fused_computation.88 | convolution fusion | flops 9663676416 | bytes 30408704 | tf_op jit(solution)/shard_map/mbtd,mbtn->dn/dot_general | solution.py:39
  795.6 17.5 %fusion.64 = f32[1024,512]{0,1:T(8,128)} fusion(bf16[2,12,384,1024]{3,2,1,0:T(8,128)(2,1)} %get-tuple-element.7, bf16[2,12,384,512]{3,2,1,0:T(8,128)(2,1)} %get-tuple-element.24), kind=kOutput, calls=%fused_computation.89 | convolution fusion | flops 9663676416 | bytes 30408704 | tf_op jit(solution)/shard_map/mbtd,mbtn->dn/dot_general | solution.py:39
  813.2 88.0 %all-reduce.8.cloned.1.call-done = bf16[2,12,384,1024]{3,2,1,0:T(8,128)(2,1)} async-done(((bf16[2,12,384,1024]{3,2,1,0:T(8,128)(2,1)}), bf16[2,12,384,1024]{3,2,1,0:T(8,128)(2,1)}) %all-reduce.8.cloned.1.call-update) | async-done | bytes 18874384 | tf_op jit(solution)/shard_map/psum | solution.py:23
  901.2 58.4 %fusion.5 = (bf16[2,12,384,1024]{3,2,1,0:T(8,128)(2,1)}, bf16[2,12,384,1024]{3,2,1,0:T(8,128)(2,1)}, bf16[2,12,384,1024]{3,2,1,0:T(8,128)(2,1)}, bf16[2,12,384,1024]{3,2,1,0:T(8,128)(2,1)}) fusion(bf16[2,12,384,1024]{3,2,1,0:T(8,128)(2,1)} %copy-done.1, bf16[2,12,384,1024]{3,2,1,0:T(8,128)(2,1)} %all-reduce.8.cloned.1.call-done, ...), kind=kLoop, calls=%fused_computation.11 | loop fusion | flops 113246208 | bytes 150995040 | tf_op jit(solution)/shard_map/convert_element_type | solution.py:30
  959.6 17.6 %fusion.74 = f32[512,1024]{1,0:T(8,128)} fusion(bf16[2,12,384,1024]{3,2,1,0:T(8,128)(2,1)} %get-tuple-element.20, bf16[2,12,384,512]{3,2,1,0:T(8,128)(2,1)} %get-tuple-element.9), kind=kOutput, calls=%fused_computation.91 | convolution fusion | flops 9663676416 | bytes 30408704 | tf_op jit(solution)/shard_map/mbtn,mbtd->nd/dot_general | solution.py:40
  977.2 17.8 %fusion.79 = f32[512,1024]{1,0:T(8,128)} fusion(bf16[2,12,384,1024]{3,2,1,0:T(8,128)(2,1)} %get-tuple-element.21, bf16[2,12,384,512]{3,2,1,0:T(8,128)(2,1)} %get-tuple-element.10), kind=kOutput, calls=%fused_computation.92 | convolution fusion | flops 9663676416 | bytes 30408704 | tf_op jit(solution)/shard_map/mbtn,mbtd->nd/dot_general | solution.py:40
  995.1 17.5 %fusion.69 = f32[512,1024]{1,0:T(8,128)} fusion(bf16[2,12,384,1024]{3,2,1,0:T(8,128)(2,1)} %get-tuple-element.13, bf16[2,12,384,512]{3,2,1,0:T(8,128)(2,1)} %get-tuple-element.11), kind=kOutput, calls=%fused_computation.90 | convolution fusion | flops 9663676416 | bytes 30408704 | tf_op jit(solution)/shard_map/mbtn,mbtd->nd/dot_general | solution.py:40
  1017.6 19.9 %reduce-scatter.11.cloned.1.call-done = f32[256,512]{0,1:T(8,128)} async-done(((f32[1024,512]{0,1:T(8,128)}), f32[256,512]{0,1:T(8,128)}) %reduce-scatter.11.cloned.1.call-update) | async-done | bytes 524304 | tf_op jit(solution)/shard_map/reduce_scatter | solution.py:41
  1040.3 42.4 %reduce-scatter.15.cloned.1.call-done = f32[512,256]{1,0:T(8,128)} async-done(((f32[512,1024]{1,0:T(8,128)}), f32[512,256]{1,0:T(8,128)}) %reduce-scatter.15.cloned.1.call-update) | async-done | bytes 524304 | tf_op jit(solution)/shard_map/reduce_scatter | solution.py:42
  1082.7 45.2 %reduce-scatter.17.cloned.1.call-done = f32[512,256]{1,0:T(8,128)} async-done(((f32[512,1024]{1,0:T(8,128)}), f32[512,256]{1,0:T(8,128)}) %reduce-scatter.17.cloned.1.call-update) | async-done | bytes 524304 | tf_op jit(solution)/shard_map/reduce_scatter | solution.py:42
  1127.9 45.2 %reduce-scatter.13.cloned.1.call-done = f32[512,256]{1,0:T(8,128)} async-done(((f32[512,1024]{1,0:T(8,128)}), f32[512,256]{1,0:T(8,128)}) %reduce-scatter.13.cloned.1.call-update) | async-done | bytes 524304 | tf_op jit(solution)/shard_map/reduce_scatter | solution.py:42
  (45 shorter events, 108.7 us)
Async XLA Ops:
  7.2 286.0 %all-reduce.4.cloned.1.call-start = ((), (), s32[]{:S(2)}) async-start(), calls=%async_computation.6 | async-start | bytes 37748736 | tf_op jit(solution)/shard_map/psum | solution.py:23
  51.6 545.3 %all-reduce.6.cloned.1.call-start = ((), (), s32[]{:S(2)}) async-start(), calls=%async_computation.7 | async-start | bytes 37748736 | tf_op jit(solution)/shard_map/psum | solution.py:23
  309.8 6.5 copy-start
  358.0 543.1 %all-reduce.8.cloned.1.call-start = ((), (), s32[]{:S(2)}) async-start(), calls=%async_computation.14 | async-start | bytes 37748736 | tf_op jit(solution)/shard_map/psum | solution.py:23
  613.5 6.3 copy-start.1
  662.0 353.4 %reduce-scatter.7.cloned.1.call-start = ((), (), s32[]{:S(2)}) async-start(), calls=%async_computation.8 | async-start | bytes 2621440 | tf_op jit(solution)/shard_map/reduce_scatter | solution.py:41
  698.1 29.1 %copy-start.2 = (f32[2,12]{1,0:T(2,128)S(1)}, f32[2,12]{1,0:T(2,128)}, u32[]{:S(2)}) copy-start(f32[2,12]{1,0:T(2,128)} %add_reduce_fusion.2) | copy-start | bytes 292
  777.8 238.7 %reduce-scatter.9.cloned.1.call-start = ((), (), s32[]{:S(2)}) async-start(), calls=%async_computation.9 | async-start | bytes 2621440 | tf_op jit(solution)/shard_map/reduce_scatter | solution.py:41
  795.6 241.9 %reduce-scatter.11.cloned.1.call-start = ((), (), s32[]{:S(2)}) async-start(), calls=%async_computation.10 | async-start | bytes 2621440 | tf_op jit(solution)/shard_map/reduce_scatter | solution.py:41
  813.2 269.5 %reduce-scatter.15.cloned.1.call-start = ((), (), s32[]{:S(2)}) async-start(), calls=%async_computation.12 | async-start | bytes 2621440 | tf_op jit(solution)/shard_map/reduce_scatter | solution.py:42
  977.2 150.7 %reduce-scatter.17.cloned.1.call-start = ((), (), s32[]{:S(2)}) async-start(), calls=%async_computation.13 | async-start | bytes 2621440 | tf_op jit(solution)/shard_map/reduce_scatter | solution.py:42
  995.0 178.1 %reduce-scatter.13.cloned.1.call-start = ((), (), s32[]{:S(2)}) async-start(), calls=%async_computation.11 | async-start | bytes 2621440 | tf_op jit(solution)/shard_map/reduce_scatter | solution.py:42
Sparse Core Ops, SparseCore 0:
  51.8 241.3 all-reduce.3
  358.2 238.7 all-reduce.5
  662.1 239.0 all-reduce.7
  903.3 44.0 reduce-scatter.6
  949.5 42.8 reduce-scatter.8
  994.6 42.8 reduce-scatter.10
  1039.8 42.8 reduce-scatter.14
  1085.0 42.8 reduce-scatter.16
  1130.2 42.8 reduce-scatter.12
where the time goes:
time: 1190 us; the launch traced here: 1180 us
  matrix products  484 us (41%)
  waiting for transfers between devices  470 us (39%)
  other arithmetic  143 us (12%)
  local copies, waits for them, and re-layouts  56.5 us (5%)
  between operations  15.7 us (1%)
  blocking collectives  13.1 us (1%)
    psum x3, waiting for transfers between devices, local_pass(): back_sum = lax.psum(part_back, 'tp')  317 us
    reduce_scatter x3, waiting for transfers between devices, local_pass(): lax.psum_scatter(down_part, 'dp', scatter_dimension=1, tiled=True)  133 us
    convert_element_type x3, other arithmetic, local_pass(): (grad_cot.astype(jnp.float32) + back_sum.astype(jnp.float32)).astype(jnp....  91.6 us
    dot_general x3, matrix products, local_pass(): jnp.einsum('mbtd,mbsd->mbts', x_layer, x_layer, preferred_element_type=jn...  88.4 us
    dot_general x3, matrix products, local_pass(): jnp.einsum('mbtd,nd->mbtn', grad_cot, w_down[layer_idx], preferred_elemen...  78.6 us
    dot_general x3, matrix products, local_pass(): jnp.einsum('mbtd,mbsd->mbts', grad_cot, grad_cot, preferred_element_type=...  65.1 us
    dot_general x3, matrix products, local_pass(): jnp.einsum('mbtn,mbsn->mbts', hidden, hidden, preferred_element_type=jnp....  53.8 us
    dot_general x3, matrix products, local_pass(): jnp.einsum('mbtd,mbtn->dn', x_layer, scaled_dh, preferred_element_type=jn...  52.8 us
  transfers between devices with their start and end apart: 9, of which 7 were waited for; matrix products, arithmetic and copies ran while one was open for 43% of the time, Pallas kernels for 0%

commit v1 on v0

v1 whole, which is shorter than its diff:
```python
import functools
import math

import jax
import jax.numpy as jnp
from jax import lax
from jax.experimental import pallas as pl
from jax.experimental.pallas import tpu as pltpu
from jax.sharding import PartitionSpec as P

F32 = jnp.float32
BF16 = jnp.bfloat16
NT = (((1,), (1,)), ((), ()))
ANY = pl.BlockSpec(memory_space=pl.ANY)
VMEM = pl.BlockSpec(memory_space=pltpu.VMEM)
LAG = 2
U_GROUP = 4
COEF = math.sqrt(2.0 / math.pi)
CUBE = 0.044715


def place():
    t = lax.axis_index("tp")
    core = lax.rem(t, 2)
    px = lax.rem(lax.div(t, 2), 2)
    py = lax.div(t, 4)
    return core, px, py, t + 2 - 4 * px, t + 4 - 8 * py, t + 1 - 2 * core


def enter(peers):
    barrier = pltpu.get_barrier_semaphore()
    for peer in peers:
        pl.semaphore_signal(barrier, inc=1, device_id={"tp": peer}, device_id_type=pl.DeviceIdType.MESH)
    pl.semaphore_wait(barrier, len(peers))


def push(src, dst, send_sem, recv_sem, peer):
    return pltpu.make_async_remote_copy(src_ref=src, dst_ref=dst, send_sem=send_sem, recv_sem=recv_sem, device_id={"tp": peer}, device_id_type=pl.DeviceIdType.MESH)


class Exchange:
    def __init__(self, pos, part, cot, got1, got2, sems, n_examples, n_slots):
        self.core, self.px, self.py, self.nx, self.ny, self.partner = pos
        self.part, self.cot, self.got1, self.got2, self.sems = part, cot, got1, got2, sems
        self.n_examples, self.n_slots = n_examples, n_slots

    def copies(self, kind, j):
        px, py = self.px, self.py
        part = self.part.at[lax.rem(j, self.n_slots)]
        cot = self.cot.at[lax.rem(j, self.n_examples)]
        s = lax.rem(j, 4)
        send, recv = self.sems.at[0, kind], self.sems.at[1, kind]
        if kind == 0:
            pairs = ((part.at[pl.ds(2 * (1 - px), 2)], self.got1.at[s, 0], self.nx), (part.at[pl.ds(4 + 2 * (1 - py), 2)], self.got1.at[s, 1], self.ny))
        elif kind == 1:
            pairs = ((part.at[2 * px + 1 - py], self.got2.at[s, 0], self.ny), (part.at[4 + 2 * py + 1 - px], self.got2.at[s, 1], self.nx))
        elif kind == 2:
            own_a, own_b = cot.at[2 * px + py], cot.at[4 + 2 * py + px]
            pairs = ((own_a, own_a, self.ny), (own_b, own_b, self.nx))
        else:
            two_a, two_b = cot.at[pl.ds(2 * px, 2)], cot.at[pl.ds(4 + 2 * py, 2)]
            pairs = ((two_a, two_a, self.nx), (two_b, two_b, self.ny))
        return [push(src, dst, send.at[s, c], recv.at[s, c], peer) for c, (src, dst, peer) in enumerate(pairs)]

    def start(self, kind, j):
        for copy in self.copies(kind, j):
            copy.start()

    def wait(self, kind, j):
        for copy in self.copies(kind, j):
            copy.wait()

    def add_first(self, j):
        self.wait(0, j)
        slot, s = lax.rem(j, self.n_slots), lax.rem(j, 4)
        for c, first in enumerate((2 * self.px, 4 + 2 * self.py)):
            for i in range(2):
                mine = self.part[slot, first + i].astype(F32) + self.got1[s, c, i].astype(F32)
                self.part[slot, first + i] = mine.astype(BF16)
        self.start(1, j)

    def add_second(self, j):
        self.wait(1, j)
        slot, s, e = lax.rem(j, self.n_slots), lax.rem(j, 4), lax.rem(j, self.n_examples)
        for c, own in enumerate((2 * self.px + self.py, 4 + 2 * self.py + self.px)):
            back = self.part[slot, own].astype(F32) + self.got2[s, c].astype(F32)
            self.cot[e, own] = (self.cot[e, own].astype(F32) + back).astype(BF16)
        self.start(2, j)

    def forward(self, j):
        self.wait(2, j)
        self.start(3, j)


def run_stages(ex, k, count, save, saved):
    def at(lag, fn):
        j = k - lag * LAG

        @pl.when(jnp.logical_and(j >= 0, j < count))
        def _():
            fn(j)

    def finish(j):
        ex.wait(3, j)
        save(j)

    at(5, saved)
    at(4, finish)
    at(3, ex.forward)
    at(2, ex.add_second)
    at(1, ex.add_first)


def backward_kernel(u, x, w_up, w_down, d_out, dx_out, dh_out, part_out, norm_out, cot, w1, w2, u_own, u_far, x_buf, d_act, hid, dh, part, got1, got2, gram_a, gram_b, sems, w_sems, u_sems, cot_sems, load_sems, dh_sems, dx_sems, all_sems, part_sems):
    n_layers, _, n_ex, seq, d_ff = u.shape
    d_model = x.shape[-1]
    pieces = cot.shape[1:]
    groups = n_ex // U_GROUP
    total = n_layers * n_ex
    summed = total - n_ex
    pos = place()
    core, partner = pos[0], pos[5]
    enter(pos[3:])
    ex = Exchange(pos, part, cot, got1, got2, sems, n_ex, 4)

    def layer_of(k):
        return n_layers - 1 - lax.div(k, n_ex)

    def weight_copies(layer):
        near = [
            pltpu.make_async_copy(w_down.at[layer], w2.at[layer, pl.ds(0, d_ff)], w_sems.at[0, layer, 0]),
            pltpu.make_async_copy(w_up.at[layer], w1.at[layer, :, pl.ds(0, d_ff)], w_sems.at[0, layer, 1]),
        ]
        far = [
            push(w_down.at[layer], w2.at[layer, pl.ds(d_ff, d_ff)], w_sems.at[1, layer, 0], w_sems.at[2, layer, 0], partner),
            push(w_up.at[layer], w1.at[layer, :, pl.ds(d_ff, d_ff)], w_sems.at[1, layer, 1], w_sems.at[2, layer, 1], partner),
        ]
        return near, far

    def far_copy(g):
        first = lax.rem(g, groups) * U_GROUP
        layer = n_layers - 1 - lax.div(g, groups)
        return push(u.at[layer, 1 - core, pl.ds(first, U_GROUP)], u_far.at[pl.ds(g * U_GROUP, U_GROUP)], u_sems.at[0, g], u_sems.at[1, g], partner)

    def cot_copy(e):
        return pltpu.make_async_copy(d_out.at[core, e], cot.at[e], cot_sems.at[e])

    def load_copies(k):
        layer, e, s = layer_of(k), lax.rem(k, n_ex), lax.rem(k, 2)
        return [
            pltpu.make_async_copy(u.at[layer, core, e], u_own.at[s], load_sems.at[s, 0]),
            pltpu.make_async_copy(x.at[layer, core, e], x_buf.at[s], load_sems.at[s, 1]),
        ]

    def dh_copies(k):
        layer, e, s = layer_of(k), lax.rem(k, n_ex), lax.rem(k, 2)
        near = pltpu.make_async_copy(dh.at[s, :, pl.ds(0, d_ff)], dh_out.at[layer, core, e], dh_sems.at[s, 0])
        far = push(dh.at[s, :, pl.ds(d_ff, d_ff)], dh_out.at[layer, core, e], dh_sems.at[s, 1], all_sems.at[0], partner)
        return near, far

    def dx_copies(j):
        step, e, s = lax.div(j, n_ex), lax.rem(j, n_ex), lax.rem(j, 4)
        near = pltpu.make_async_copy(cot.at[e], dx_out.at[step, core, e], dx_sems.at[s, 0])
        far = push(cot.at[e], dx_out.at[step, core, e], dx_sems.at[s, 1], all_sems.at[1], partner)
        return near, far

    def part_copy(k):
        s = lax.rem(k, 4)
        return pltpu.make_async_copy(part.at[s], part_out.at[lax.rem(k, n_ex)], part_sems.at[s])

    def save(j):
        for copy in dx_copies(j):
            copy.start()

    def saved(j):
        near, far = dx_copies(j)
        near.wait()
        far.wait_send()

    top = n_layers - 1
    near, far = weight_copies(top)
    near[0].start()
    far[0].start()
    far_copy(0).start()
    cot_copy(0).start()
    for copy in load_copies(0):
        copy.start()
    near[1].start()
    far[1].start()

    @pl.loop(1, n_ex)
    def _(e):
        cot_copy(e).start()

    for layer in reversed(range(top)):
        for copy in sum(weight_copies(layer), []):
            copy.start()

    @pl.loop(1, n_layers * groups)
    def _(g):
        far_copy(g).start()

    norm_out[...] = jnp.zeros_like(norm_out)

    def compute(k):
        layer, e, s = layer_of(k), lax.rem(k, n_ex), lax.rem(k, 2)

        @pl.when(lax.rem(k, n_ex) == 0)
        def _():
            near, far = weight_copies(layer)
            for copy in near:
                copy.wait()
            for copy in far:
                copy.wait_recv()

        @pl.when(lax.rem(k, U_GROUP) == 0)
        def _():
            far_copy(lax.div(k, U_GROUP)).wait_recv()

        @pl.when(k < n_ex)
        def _():
            cot_copy(e).wait()

        for copy in load_copies(k):
            copy.wait()

        @pl.when(k + 1 < total)
        def _():
            for copy in load_copies(k + 1):
                copy.start()

        @pl.when(k >= 2)
        def _():
            near, far = dh_copies(k - 2)
            near.wait()
            far.wait_send()

        d_act[...] = lax.dot_general(cot[e].reshape(seq, d_model), w2[layer], NT, preferred_element_type=F32)
        rows = 32

        @pl.loop(0, seq // rows)
        def _(r):
            at = pl.ds(pl.multiple_of(r * rows, rows), rows)
            for half in range(2):
                columns = pl.ds(half * d_ff, d_ff)
                v = (u_own[s, at] if half == 0 else u_far[k, at]).astype(F32)
                square = v * v
                t = jnp.tanh(COEF * (v + CUBE * (square * v)))
                gate = 0.5 * (1.0 + t)
                slope = gate + (0.5 * v) * (1.0 - t * t) * (COEF * (1.0 + (3.0 * CUBE) * square))
                hid[at, columns] = (v * gate).astype(BF16)
                dh[s, at, columns] = (slope * d_act[at, columns]).astype(BF16)

        for copy in dh_copies(k):
            copy.start()
        back = lax.dot_general(dh[s], w1[layer], NT, preferred_element_type=F32)
        part[lax.rem(k, 4)] = back.astype(BF16).reshape(pieces)

        @pl.when(k < summed)
        def _():
            ex.start(0, k)

        @pl.when(k >= summed)
        def _():
            part_copy(k).start()

        for left, right in ((hid[...], cot[e].reshape(seq, d_model)), (x_buf[s], dh[s])):
            gram_a[...] = lax.dot_general(left, left, NT, preferred_element_type=F32)
            gram_b[...] = lax.dot_general(right, right, NT, preferred_element_type=F32)
            norm_out[e] += jnp.sum((gram_a[...] * gram_b[...]).reshape(seq // 8, 8, seq), axis=0)

    def iteration(k):
        run_stages(ex, k, summed, save, saved)

        @pl.when(jnp.logical_and(k >= summed + LAG, k < total + LAG))
        def _():
            part_copy(k - LAG).wait()

        @pl.when(k < total)
        def _():
            compute(k)

    @pl.loop(0, max(total + LAG, summed + 5 * LAG))
    def _(k):
        iteration(k)

    for k in (total - 2, total - 1):
        near, far = dh_copies(k)
        near.wait()
        far.wait_send()
    pltpu.make_async_copy(dh_out.at[:, 1 - core], dh_out.at[:, 1 - core], all_sems.at[0]).wait()
    pltpu.make_async_copy(dx_out.at[:, 1 - core], dx_out.at[:, 1 - core], all_sems.at[1]).wait()
    for layer in range(n_layers):
        for copy in weight_copies(layer)[1]:
            copy.wait_send()

    @pl.loop(0, n_layers * groups)
    def _(g):
        far_copy(g).wait_send()


def backward_call(u, x, w_up, w_down, d_out):
    n_layers, _, n_ex, seq, d_ff = u.shape
    d_model = x.shape[-1]
    pieces = (8, seq // 8, d_model)
    total = n_layers * n_ex
    rows = total * seq
    dma = pltpu.SemaphoreType.DMA
    return pl.pallas_call(
        backward_kernel,
        out_shape=(
            jax.ShapeDtypeStruct((n_layers - 1, 2, n_ex) + pieces, BF16),
            jax.ShapeDtypeStruct((n_layers, 2, n_ex, seq, d_ff), BF16),
            jax.ShapeDtypeStruct((n_ex,) + pieces, BF16),
            jax.ShapeDtypeStruct((n_ex, 8, seq), F32),
        ),
        in_specs=[ANY] * 5,
        out_specs=(ANY, ANY, ANY, VMEM),
        scratch_shapes=[
            pltpu.VMEM((n_ex,) + pieces, BF16),
            pltpu.VMEM((n_layers, d_model, 2 * d_ff), BF16),
            pltpu.VMEM((n_layers, 2 * d_ff, d_model), BF16),
            pltpu.VMEM((2, seq, d_ff), BF16),
            pltpu.VMEM((total, seq, d_ff), BF16),
            pltpu.VMEM((2, seq, d_model), BF16),
            pltpu.VMEM((seq, 2 * d_ff), F32),
            pltpu.VMEM((seq, 2 * d_ff), BF16),
            pltpu.VMEM((2, seq, 2 * d_ff), BF16),
            pltpu.VMEM((4,) + pieces, BF16),
            pltpu.VMEM((4, 2, 2) + pieces[1:], BF16),
            pltpu.VMEM((4, 2) + pieces[1:], BF16),
            pltpu.VMEM((seq, seq), F32),
            pltpu.VMEM((seq, seq), F32),
            dma((2, 4, 4, 2)),
            dma((3, n_layers, 2)),
            dma((2, total // U_GROUP)),
            dma((n_ex,)),
            dma((2, 2)),
            dma((2, 2)),
            dma((4, 2)),
            dma((2,)),
            dma((4,)),
        ],
        compiler_params=pltpu.CompilerParams(collective_id=0, has_side_effects=True, vmem_limit_bytes=66_000_000),
        cost_estimate=pl.CostEstimate(flops=rows * d_model * d_ff * 16, bytes_accessed=rows * d_model * 16, transcendentals=rows * d_ff * 2),
        name="backward",
    )(u, x, w_up, w_down, d_out.reshape((2, n_ex) + pieces))


def sum_kernel(part_in, cot_in, dx_out, cot, part, got1, got2, sems, in_sems, dx_sems, all_sems):
    n_ex = part_in.shape[0]
    pos = place()
    core, partner = pos[0], pos[5]
    enter(pos[3:])
    ex = Exchange(pos, part, cot, got1, got2, sems, n_ex, n_ex)

    def in_copies(e):
        return [
            pltpu.make_async_copy(part_in.at[e], part.at[e], in_sems.at[e, 0]),
            pltpu.make_async_copy(cot_in.at[core, e], cot.at[e], in_sems.at[e, 1]),
        ]

    def dx_copies(j):
        s = lax.rem(j, 4)
        near = pltpu.make_async_copy(cot.at[j], dx_out.at[core, j], dx_sems.at[s, 0])
        far = push(cot.at[j], dx_out.at[core, j], dx_sems.at[s, 1], all_sems.at[0], partner)
        return near, far

    def save(j):
        for copy in dx_copies(j):
            copy.start()

    def saved(j):
        near, far = dx_copies(j)
        near.wait()
        far.wait_send()

    @pl.loop(0, n_ex)
    def _(e):
        for copy in in_copies(e):
            copy.start()

    @pl.loop(0, n_ex + 5 * LAG)
    def _(k):
        run_stages(ex, k, n_ex, save, saved)

        @pl.when(k < n_ex)
        def _():
            for copy in in_copies(k):
                copy.wait()
            ex.start(0, k)

    pltpu.make_async_copy(dx_out.at[1 - core], dx_out.at[1 - core], all_sems.at[0]).wait()


def sum_call(part, cot):
    n_ex = part.shape[0]
    pieces = part.shape[1:]
    dma = pltpu.SemaphoreType.DMA
    return pl.pallas_call(
        sum_kernel,
        out_shape=jax.ShapeDtypeStruct((2, n_ex) + pieces, BF16),
        in_specs=[ANY] * 2,
        out_specs=ANY,
        scratch_shapes=[
            pltpu.VMEM((n_ex,) + pieces, BF16),
            pltpu.VMEM((n_ex,) + pieces, BF16),
            pltpu.VMEM((4, 2, 2) + pieces[1:], BF16),
            pltpu.VMEM((4, 2) + pieces[1:], BF16),
            dma((2, 4, 4, 2)),
            dma((n_ex, 2)),
            dma((4, 2)),
            dma((1,)),
        ],
        compiler_params=pltpu.CompilerParams(collective_id=1, has_side_effects=True, vmem_limit_bytes=40_000_000),
        cost_estimate=pl.CostEstimate(flops=200_000_000_000, bytes_accessed=part.size * 8, transcendentals=0),
        name="sum_rows",
    )(part, cot)


def solution(mesh):
    dp_size = mesh.shape["dp"]

    def local_pass(x_in, u_pre, w_up, w_down, d_out, noise_up, noise_down, clip_norm, noise_mult):
        n_layers = x_in.shape[0]
        examples = d_out.shape[0] * d_out.shape[1] * dp_size
        core = lax.rem(lax.axis_index("tp"), 2)
        dx, dh, part, norms = backward_call(u_pre, x_in, w_up, w_down, d_out)
        own_norm = jnp.sum(norms, axis=(1, 2))
        norm_part = jnp.where(jnp.arange(2)[:, None] == core, own_norm[None, :], 0.0)
        norm_vec = lax.psum(norm_part, "tp")
        clip_col = jnp.minimum(1.0, clip_norm[0] / jnp.sqrt(norm_vec))[:, :, None, None]
        noise_scale = noise_mult[0] * clip_norm[0]
        up_parts, down_parts = [], []
        for layer_idx in range(n_layers):
            if layer_idx == n_layers - 1:
                cot_layer = d_out
            else:
                cot_layer = dx[n_layers - 2 - layer_idx].reshape(d_out.shape)
            hidden = jax.nn.gelu(u_pre[layer_idx].astype(F32)).astype(BF16)
            scaled_dh = (dh[layer_idx] * clip_col).astype(BF16)
            scaled_cot = (cot_layer * clip_col).astype(BF16)
            up_parts.append(jnp.einsum("mbtd,mbtn->dn", x_in[layer_idx], scaled_dh, preferred_element_type=F32))
            down_parts.append(jnp.einsum("mbtn,mbtd->nd", hidden, scaled_cot, preferred_element_type=F32))
        late_part, _ = lax.optimization_barrier((part, (up_parts, down_parts)))
        d_in = sum_call(late_part, dx[n_layers - 2]).reshape(d_out.shape)
        up_grads, down_grads = [], []
        for layer_idx in range(n_layers):
            up_sum = lax.psum_scatter(up_parts[layer_idx], "dp", scatter_dimension=0, tiled=True)
            down_sum = lax.psum_scatter(down_parts[layer_idx], "dp", scatter_dimension=1, tiled=True)
            up_grads.append((up_sum + noise_scale * noise_up[layer_idx]) / examples)
            down_grads.append((down_sum + noise_scale * noise_down[layer_idx]) / examples)
        return jnp.stack(up_grads), jnp.stack(down_grads), d_in

    in_specs = (P(None, None, "dp", None, None), P(None, None, "dp", None, "tp"), P(None, None, "tp"), P(None, "tp", None), P(None, "dp", None, None), P(None, "dp", "tp"), P(None, "tp", "dp"), P(), P())
    out_specs = (P(None, "dp", "tp"), P(None, "tp", "dp"), P(None, "dp", None, None))
    return jax.shard_map(local_pass, mesh=mesh, in_specs=in_specs, out_specs=out_specs, check_vma=False)
```

time: 1190 us -> 849 us (0.71)
  Pallas kernels: 0 us -> 521 us
  waiting for transfers between devices: 470 us -> 0.17 us
  matrix products: 484 us -> 105 us
  other arithmetic: 143 us -> 100 us
  local copies, waits for them, and re-layouts: 56.5 us -> 93.9 us
    pallas_call x0 -> x2, Pallas kernels: none -> 521 us  [the longest x1 363 us: backward_call(): pl.pallas_call(backward_kernel, out_shape=(jax.ShapeDtypeStruct((n_layers...]
    dot_general x24 -> x6, matrix products: 484 us -> 105 us  [the longest x3 52.6 us: local_pass(): jnp.einsum('mbtd,mbtn->dn', x_in[layer_idx], scaled_dh, preferred_element...]
    psum x3 -> x0, waiting for transfers between devices: 317 us -> none  [local_pass(): back_sum = lax.psum(part_back, 'tp')]
    reduce_scatter x6, waiting for transfers between devices: 153 us -> 0.07 us  [the longest x3 0.06 us: local_pass(): lax.psum_scatter(up_parts[layer_idx], 'dp', scatter_dimension=0, tiled=True)]
    convert_element_type x5 -> x3, other arithmetic: 136 us -> 92.2 us  [the longest x1 47.7 us: local_pass(): scaled_cot = (cot_layer * clip_col).astype(BF16)]
    slice x1 -> x2, local copies, waits for them, and re-layouts: 1.48 us -> 40.3 us  [the longest x1 40.1 us: local_pass(): x_in[layer_idx]]
  transfers between devices with their start and end apart: 9 -> 6, of which waited for: 7 -> 0; matrix products, arithmetic and copies ran while one was open for 43% -> 23% of each run, Pallas kernels for 0% -> 19%
where the time goes in v1:
time: 849 us; the launch traced here: 848 us
  Pallas kernels  521 us (61%)
  matrix products  105 us (12%)
  other arithmetic  100 us (12%)
  local copies, waits for them, and re-layouts  93.9 us (11%)
  between operations  15.5 us (2%)
  blocking collectives  11.8 us (1%)
    pallas_call x1, Pallas kernels, backward_call(): pl.pallas_call(backward_kernel, out_shape=(jax.ShapeDtypeStruct((n_layers...  363 us
    pallas_call x1, Pallas kernels, sum_call(): pl.pallas_call(sum_kernel, out_shape=jax.ShapeDtypeStruct((2, n_ex) + pie...  158 us
    dot_general x3, matrix products, local_pass(): jnp.einsum('mbtd,mbtn->dn', x_in[layer_idx], scaled_dh, preferred_element...  52.6 us
    dot_general x3, matrix products, local_pass(): jnp.einsum('mbtn,mbtd->nd', hidden, scaled_cot, preferred_element_type=F32)  52.5 us
    convert_element_type x1, other arithmetic, local_pass(): scaled_cot = (cot_layer * clip_col).astype(BF16)  47.7 us
    slice x1, local copies, waits for them, and re-layouts, local_pass(): x_in[layer_idx]  40.1 us
    squeeze x1, local copies, waits for them, and re-layouts, local_pass(): d_in = sum_call(late_part, dx[n_layers - 2]).reshape(d_out.shape)  31.1 us
    convert_element_type x1, other arithmetic, local_pass(): hidden = jax.nn.gelu(u_pre[layer_idx].astype(F32)).astype(BF16)  25.3 us
  transfers between devices with their start and end apart: 6, of which 0 were waited for; matrix products, arithmetic and copies ran while one was open for 23% of the time, Pallas kernels for 19%

profile of v1, /device:TPU:0, one launch (start us, length us, event | category | flops | bytes accessed | tf_op | source)
XLA Modules:
  0.0 848.4 jit_solution(6346895538991646278)
XLA Ops:
  7.2 362.8 %backward.1 = (bf16[2,2,12,8,48,1024]{5,4,3,2,1,0:T(8,128)(2,1)}, bf16[3,2,12,384,512]{4,3,2,1,0:T(8,128)(2,1)}, bf16[12,8,48,1024]{3,2,1,0:T(8,128)(2,1)}, f32[12,8,384]{2,1,0:T(8,128)}) custom-call(bf16[3,2,12,384,512]{4,3,2,1,0:T(8,128)(2,1)} %u.1, bf16[3,2,12,384,1024]{4,3,2,1,0:T(8,128)(2,1)} %x.1, bf16[3,1024,512]{2,1,0:T(8,128)(2,1)} %w_up.1, ...), custom_call_target="tpu_custom_call" | custom-call | flops 115964116992 | bytes 226492416 | tf_op jit(solution)/shard_map/backward/pallas_call | solution.py:309
  370.0 1.1 reduce_sum.9
  371.1 0.1 broadcast_select_fusion
  371.1 40.1 %fusion.74 = (bf16[1,2,12,384,1024]{4,3,2,1,0:T(8,128)(2,1)}, bf16[1,2,12,384,1024]{4,3,2,1,0:T(8,128)(2,1)}, bf16[1,2,12,384,1024]{4,3,2,1,0:T(8,128)(2,1)}) fusion(bf16[3,2,12,384,1024]{4,3,2,1,0:T(8,128)(2,1)} %x.1), kind=kLoop, calls=%fused_computation.89 | loop fusion | bytes 113246208 | tf_op jit(solution)/shard_map/slice | solution.py:443
  411.3 11.8 %psum.7 = f32[2,12]{1,0:T(2,128)S(1)} all-reduce(f32[2,12]{1,0:T(2,128)S(1)} %broadcast_select_fusion), channel_id=1, replica_groups=mesh['dp'=4,'tp'=8] {'tp'}, use_global_device_ids=true, to_apply=%region_1.2 | all-reduce | flops 24 | bytes 192 | tf_op jit(solution)/shard_map/psum | solution.py:431
  423.7 19.2 %fusion.25 = (bf16[2,12,384,512]{3,2,1,0:T(8,128)(2,1)}, bf16[2,12,384,512]{3,2,1,0:T(8,128)(2,1)}, bf16[2,12,384,512]{3,2,1,0:T(8,128)(2,1)}) fusion(f32[2,12]{1,0:T(2,128)S(1)} %multiply_minimum_fusion, bf16[3,2,12,384,512]{4,3,2,1,0:T(8,128)(2,1)} %get-tuple-element.8), kind=kLoop, calls=%fused_computation.46 | loop fusion | flops 42467328 | bytes 56623200 | tf_op jit(solution)/shard_map/convert_element_type | solution.py:441
  442.9 17.5 %fusion.53 = f32[1024,512]{0,1:T(8,128)} fusion(bf16[1,2,12,384,1024]{4,3,2,1,0:T(8,128)(2,1)} %get-tuple-element.16, bf16[2,12,384,512]{3,2,1,0:T(8,128)(2,1)} %get-tuple-element.22), kind=kOutput, calls=%fused_computation.62 | convolution fusion | flops 9663676416 | bytes 30408704 | tf_op jit(solution)/shard_map/mbtd,mbtn->dn/dot_general | solution.py:443
  460.4 0.2 reduce-scatter.9.cloned.1.call-start
  460.6 17.5 %fusion.56 = f32[1024,512]{0,1:T(8,128)} fusion(bf16[1,2,12,384,1024]{4,3,2,1,0:T(8,128)(2,1)} %get-tuple-element.17, bf16[2,12,384,512]{3,2,1,0:T(8,128)(2,1)} %get-tuple-element.23), kind=kOutput, calls=%fused_computation.63 | convolution fusion | flops 9663676416 | bytes 30408704 | tf_op jit(solution)/shard_map/mbtd,mbtn->dn/dot_general | solution.py:443
  478.2 17.6 %fusion.59 = f32[1024,512]{0,1:T(8,128)} fusion(bf16[1,2,12,384,1024]{4,3,2,1,0:T(8,128)(2,1)} %get-tuple-element.18, bf16[2,12,384,512]{3,2,1,0:T(8,128)(2,1)} %get-tuple-element.24), kind=kOutput, calls=%fused_computation.64 | convolution fusion | flops 9663676416 | bytes 30408704 | tf_op jit(solution)/shard_map/mbtd,mbtn->dn/dot_general | solution.py:443
  495.9 0.3 reduce-scatter.13.cloned.1.call-start
  496.1 31.1 %slice_bitcast_fusion = (bf16[2,12,8,48,1024]{4,3,2,1,0:T(8,128)(2,1)}, bf16[1,2,12,8,48,1024]{5,4,3,2,1,0:T(8,128)(2,1)}, bf16[1,2,12,8,48,1024]{5,4,3,2,1,0:T(8,128)(2,1)}) fusion(bf16[2,2,12,8,48,1024]{5,4,3,2,1,0:T(8,128)(2,1)} %get-tuple-element.10), kind=kLoop, calls=%fused_computation.88 | loop fusion | bytes 94371840 | tf_op jit(solution)/shard_map/squeeze | solution.py:446
  527.3 47.7 %fusion.1 = (bf16[2,12,384,1024]{3,2,1,0:T(8,128)(2,1)}, bf16[2,12,384,1024]{3,2,1,0:T(8,128)(2,1)}, bf16[2,12,384,1024]{3,2,1,0:T(8,128)(2,1)}) fusion(bf16[2,12,384,1024]{3,2,1,0:T(8,128)(2,1)} %bitcast.125, f32[2,12]{1,0:T(2,128)S(1)} %multiply_minimum_fusion, bf16[2,12,384,1024]{3,2,1,0:T(8,128)(2,1)} %bitcast.124, bf16[2,12,384,1024]{3,2,1,0:T(8,128)(2,1)} %param.13), kind=kLoop, calls=%fused_computation.3 | loop fusion | flops 84934656 | bytes 113246304 | tf_op jit(solution)/shard_map/convert_element_type | solution.py:442
  575.0 25.3 %fusion.7 = (bf16[2,12,384,512]{3,2,1,0:T(8,128)(2,1)}, bf16[2,12,384,512]{3,2,1,0:T(8,128)(2,1)}, bf16[2,12,384,512]{3,2,1,0:T(8,128)(2,1)}) fusion(bf16[3,2,12,384,512]{4,3,2,1,0:T(8,128)(2,1)} %u.1), kind=kLoop, calls=%fused_computation.22 | loop fusion | flops 141557760 | bytes 56623104 | tf_op jit(solution)/shard_map/convert_element_type | solution.py:440
  600.3 17.5 %fusion.38 = f32[512,1024]{1,0:T(8,128)} fusion(bf16[2,12,384,1024]{3,2,1,0:T(8,128)(2,1)} %get-tuple-element.34, bf16[2,12,384,512]{3,2,1,0:T(8,128)(2,1)} %get-tuple-element.25), kind=kOutput, calls=%fused_computation.59 | convolution fusion | flops 9663676416 | bytes 30408704 | tf_op jit(solution)/shard_map/mbtn,mbtd->nd/dot_general | solution.py:444
  617.8 0.3 reduce-scatter.15.cloned.1.call-start
  618.1 17.5 %fusion.43 = f32[512,1024]{1,0:T(8,128)} fusion(bf16[2,12,384,1024]{3,2,1,0:T(8,128)(2,1)} %get-tuple-element.35, bf16[2,12,384,512]{3,2,1,0:T(8,128)(2,1)} %get-tuple-element.27), kind=kOutput, calls=%fused_computation.60 | convolution fusion | flops 9663676416 | bytes 30408704 | tf_op jit(solution)/shard_map/mbtn,mbtd->nd/dot_general | solution.py:444
  635.7 17.6 %fusion.48 = f32[512,1024]{1,0:T(8,128)} fusion(bf16[2,12,384,1024]{3,2,1,0:T(8,128)(2,1)} %get-tuple-element.36, bf16[2,12,384,512]{3,2,1,0:T(8,128)(2,1)} %get-tuple-element.26), kind=kOutput, calls=%fused_computation.61 | convolution fusion | flops 9663676416 | bytes 30408704 | tf_op jit(solution)/shard_map/mbtn,mbtd->nd/dot_general | solution.py:444
  653.3 3.7 copy-done
  657.0 158.1 %sum_rows.1 = bf16[2,12,8,48,1024]{4,3,2,1,0:T(8,128)(2,1)} custom-call(bf16[12,8,48,1024]{3,2,1,0:T(8,128)(2,1)S(1)} %copy-done, bf16[2,12,8,48,1024]{4,3,2,1,0:T(8,128)(2,1)} %get-tuple-element.19.cot_in), custom_call_target="tpu_custom_call" | custom-call | flops 199999995904 | bytes 37748736 | tf_op jit(solution)/shard_map/sum_rows/pallas_call | solution.py:400
  815.7 0.1 fusion.75
  815.8 0.2 copy.47
  816.1 0.2 copy.49
  816.3 0.2 copy.51
  816.5 1.1 fusion.73
  817.6 1.1 fusion.71
  818.8 1.1 fusion.69
  819.9 0.1 pad_maximum_fusion
  820.0 1.6 copy.27
  821.6 2.0 fusion.67
  823.7 1.2 pad_maximum_fusion.1
  824.9 16.6 %copy.103 = bf16[2,12,384,1024]{3,2,1,0:T(8,128)(2,1)} copy(bf16[2,12,384,1024]{3,2,1,0:T(8,128)(2,1)} %bitcast.126) | data formatting | bytes 37748736
  (20 shorter events, 0.3 us)
Async XLA Ops:
  7.2 809.3 %reduce-scatter.7.cloned.1.call-start = ((), (), s32[]{:S(2)}) async-start(), calls=%async_computation.6 | async-start | bytes 2621440 | tf_op jit(solution)/shard_map/reduce_scatter | solution.py:449
  460.4 357.2 %reduce-scatter.9.cloned.1.call-start = ((), (), s32[]{:S(2)}) async-start(), calls=%async_computation.7 | async-start | bytes 2621440 | tf_op jit(solution)/shard_map/reduce_scatter | solution.py:449
  478.2 340.6 %reduce-scatter.11.cloned.1.call-start = ((), (), s32[]{:S(2)}) async-start(), calls=%async_computation.8 | async-start | bytes 2621440 | tf_op jit(solution)/shard_map/reduce_scatter | solution.py:449
  495.9 325.8 %reduce-scatter.13.cloned.1.call-start = ((), (), s32[]{:S(2)}) async-start(), calls=%async_computation.9 | async-start | bytes 2621440 | tf_op jit(solution)/shard_map/reduce_scatter | solution.py:450
  617.8 203.8 %reduce-scatter.15.cloned.1.call-start = ((), (), s32[]{:S(2)}) async-start(), calls=%async_computation.10 | async-start | bytes 2621440 | tf_op jit(solution)/shard_map/reduce_scatter | solution.py:450
  635.6 186.0 %reduce-scatter.17.cloned.1.call-start = ((), (), s32[]{:S(2)}) async-start(), calls=%async_computation.11 | async-start | bytes 2621440 | tf_op jit(solution)/shard_map/reduce_scatter | solution.py:450
  653.3 3.7 copy-start
  657.0 158.8 %copy-start.1 = (f32[3,256,512]{2,1,0:T(8,128)S(1)}, f32[3,256,512]{2,1,0:T(8,128)}, u32[]{:S(2)}) copy-start(f32[3,256,512]{2,1,0:T(8,128)} %param.14) | copy-start | bytes 4718596
Sparse Core Ops, SparseCore 0:
  460.5 43.3 reduce-scatter.6
  506.2 42.8 reduce-scatter.8
  551.4 42.8 reduce-scatter.10
  617.9 43.3 reduce-scatter.12
  663.5 42.8 reduce-scatter.14
  708.5 42.8 reduce-scatter.16

commit v2 on v1

--- a/solution.py
+++ b/solution.py
@@ -13,7 +13,7 @@
 NT = (((1,), (1,)), ((), ()))
 ANY = pl.BlockSpec(memory_space=pl.ANY)
 VMEM = pl.BlockSpec(memory_space=pltpu.VMEM)
-LAG = 2
+LAG = 1
 U_GROUP = 4
 COEF = math.sqrt(2.0 / math.pi)
 CUBE = 0.044715
@@ -145,15 +145,17 @@
     def cot_copy(e):
         return pltpu.make_async_copy(d_out.at[core, e], cot.at[e], cot_sems.at[e])
 
-    def load_copies(k):
-        layer, e, s = layer_of(k), lax.rem(k, n_ex), lax.rem(k, 2)
+    def load_copies(p):
+        k, s = example_at(p), lax.rem(p, 2)
+        layer, e = layer_of(k), lax.rem(k, n_ex)
         return [
             pltpu.make_async_copy(u.at[layer, core, e], u_own.at[s], load_sems.at[s, 0]),
             pltpu.make_async_copy(x.at[layer, core, e], x_buf.at[s], load_sems.at[s, 1]),
         ]
 
-    def dh_copies(k):
-        layer, e, s = layer_of(k), lax.rem(k, n_ex), lax.rem(k, 2)
+    def dh_copies(p):
+        k, s = example_at(p), lax.rem(p, 2)
+        layer, e = layer_of(k), lax.rem(k, n_ex)
         near = pltpu.make_async_copy(dh.at[s, :, pl.ds(0, d_ff)], dh_out.at[layer, core, e], dh_sems.at[s, 0])
         far = push(dh.at[s, :, pl.ds(d_ff, d_ff)], dh_out.at[layer, core, e], dh_sems.at[s, 1], all_sems.at[0], partner)
         return near, far
@@ -165,8 +167,19 @@
         return near, far
 
     def part_copy(k):
-        s = lax.rem(k, 4)
-        return pltpu.make_async_copy(part.at[s], part_out.at[lax.rem(k, n_ex)], part_sems.at[s])
+        s = lax.rem(k, 2)
+        return pltpu.make_async_copy(part.at[4 + s], part_out.at[lax.rem(k, n_ex)], part_sems.at[s])
+
+    early = summed - n_ex + 4 * LAG + 1
+
+    def first_of(i):
+        return jnp.where(i <= early, i, jnp.where(i < summed, 2 * i - early, i + summed - early))
+
+    def example_at(p):
+        r = p - early
+        half = lax.div(r, 2)
+        mixed = jnp.where(lax.rem(r, 2) == 0, early + half, summed + half)
+        return jnp.where(jnp.logical_or(r < 0, p >= 2 * summed - early), p, mixed)
 
     def save(j):
         for copy in dx_copies(j):
@@ -202,8 +215,9 @@
 
     norm_out[...] = jnp.zeros_like(norm_out)
 
-    def compute(k):
-        layer, e, s = layer_of(k), lax.rem(k, n_ex), lax.rem(k, 2)
+    def compute(p):
+        k, s = example_at(p), lax.rem(p, 2)
+        layer, e = layer_of(k), lax.rem(k, n_ex)
 
         @pl.when(lax.rem(k, n_ex) == 0)
         def _():
@@ -221,19 +235,23 @@
         def _():
             cot_copy(e).wait()
 
-        for copy in load_copies(k):
+        for copy in load_copies(p):
             copy.wait()
 
-        @pl.when(k + 1 < total)
-        def _():
-            for copy in load_copies(k + 1):
+        @pl.when(p + 1 < total)
+        def _():
+            for copy in load_copies(p + 1):
                 copy.start()
 
-        @pl.when(k >= 2)
-        def _():
-            near, far = dh_copies(k - 2)
+        @pl.when(p >= 2)
+        def _():
+            near, far = dh_copies(p - 2)
             near.wait()
             far.wait_send()
+
+        @pl.when(k >= summed + 2)
+        def _():
+            part_copy(k - 2).wait()
 
         d_act[...] = lax.dot_general(cot[e].reshape(seq, d_model), w2[layer], NT, preferred_element_type=F32)
         rows = 32
@@ -251,10 +269,10 @@
                 hid[at, columns] = (v * gate).astype(BF16)
                 dh[s, at, columns] = (slope * d_act[at, columns]).astype(BF16)
 
-        for copy in dh_copies(k):
+        for copy in dh_copies(p):
             copy.start()
         back = lax.dot_general(dh[s], w1[layer], NT, preferred_element_type=F32)
-        part[lax.rem(k, 4)] = back.astype(BF16).reshape(pieces)
+        part[jnp.where(k < summed, lax.rem(k, 4), 4 + lax.rem(k, 2))] = back.astype(BF16).reshape(pieces)
 
         @pl.when(k < summed)
         def _():
@@ -269,21 +287,16 @@
             gram_b[...] = lax.dot_general(right, right, NT, preferred_element_type=F32)
             norm_out[e] += jnp.sum((gram_a[...] * gram_b[...]).reshape(seq // 8, 8, seq), axis=0)
 
-    def iteration(k):
-        run_stages(ex, k, summed, save, saved)
-
-        @pl.when(jnp.logical_and(k >= summed + LAG, k < total + LAG))
-        def _():
-            part_copy(k - LAG).wait()
-
-        @pl.when(k < total)
-        def _():
-            compute(k)
-
-    @pl.loop(0, max(total + LAG, summed + 5 * LAG))
-    def _(k):
-        iteration(k)
-
+    @pl.loop(0, summed + 5 * LAG)
+    def _(i):
+        run_stages(ex, i, summed, save, saved)
+
+        @pl.loop(first_of(i), first_of(i + 1))
+        def _(p):
+            compute(p)
+
+    for k in (total - 2, total - 1):
+        part_copy(k).wait()
     for k in (total - 2, total - 1):
         near, far = dh_copies(k)
         near.wait()
@@ -326,7 +339,7 @@
             pltpu.VMEM((seq, 2 * d_ff), F32),
             pltpu.VMEM((seq, 2 * d_ff), BF16),
             pltpu.VMEM((2, seq, 2 * d_ff), BF16),
-            pltpu.VMEM((4,) + pieces, BF16),
+            pltpu.VMEM((6,) + pieces, BF16),
             pltpu.VMEM((4, 2, 2) + pieces[1:], BF16),
             pltpu.VMEM((4, 2) + pieces[1:], BF16),
             pltpu.VMEM((seq, seq), F32),
@@ -339,7 +352,7 @@
             dma((2, 2)),
             dma((4, 2)),
             dma((2,)),
-            dma((4,)),
+            dma((2,)),
         ],
         compiler_params=pltpu.CompilerParams(collective_id=0, has_side_effects=True, vmem_limit_bytes=66_000_000),
         cost_estimate=pl.CostEstimate(flops=rows * d_model * d_ff * 16, bytes_accessed=rows * d_model * 16, transcendentals=rows * d_ff * 2),
@@ -347,23 +360,88 @@
     )(u, x, w_up, w_down, d_out.reshape((2, n_ex) + pieces))
 
 
-def sum_kernel(part_in, cot_in, dx_out, cot, part, got1, got2, sems, in_sems, dx_sems, all_sems):
-    n_ex = part_in.shape[0]
+def gelu(v):
+    return v * (0.5 * (1.0 + jnp.tanh(COEF * (v + CUBE * (v * v * v)))))
+
+
+class Ring:
+    def __init__(self, size, sums, got, sems, out):
+        z = lax.axis_index("dp")
+        self.z, self.size = z, size
+        self.peers = lax.rem(z + 1, size), lax.rem(z + size - 1, size)
+        self.sums, self.got, self.sems, self.out = sums, got, sems, out
+
+    def tile(self, step, way):
+        if way == 0:
+            return 2 * lax.rem(self.z + 2 * self.size - 1 - step, self.size)
+        return 2 * lax.rem(self.z + 1 + step, self.size) + 1
+
+    def copies(self, step, j):
+        s = lax.rem(j, 4)
+        block = self.sums.at[lax.rem(lax.div(j, 4), 3), lax.rem(j, 4)]
+        return [
+            pltpu.make_async_remote_copy(
+                src_ref=block.at[self.tile(step, way)],
+                dst_ref=self.got.at[step, s, way],
+                send_sem=self.sems.at[0, step, s, way],
+                recv_sem=self.sems.at[1, step, s, way],
+                device_id={"dp": self.peers[way]},
+                device_id_type=pl.DeviceIdType.MESH,
+            )
+            for way in range(2)
+        ]
+
+    def start(self, step, j):
+        for copy in self.copies(step, j):
+            copy.start()
+
+    def add(self, step, j):
+        for copy in self.copies(step, j):
+            copy.wait()
+        g, q, s = lax.div(j, 4), lax.rem(j, 4), lax.rem(j, 4)
+        for way in range(2):
+            at = lax.rem(g, 3), q, self.tile(step + 1, way)
+            total = self.sums[at] + self.got[step, s, way]
+            if step + 1 < self.size - 1:
+                self.sums[at] = total
+            else:
+                rows, columns = total.shape
+                self.out[g, pl.ds(pl.multiple_of(q * rows, rows), rows), pl.ds(way * columns, columns)] = total
+        if step + 1 < self.size - 1:
+            self.start(step + 1, j)
+
+
+def gradient_kernel(size, part_in, dx_in, d_out, x, dh, u, clip, d_in, grads, cot, part, got1, got2, sums, got_z, a_buf, b_buf, a_scaled, b_scaled, sems, in_sems, dx_sems, all_sems, z_sems, load_sems):
+    n_layers, _, n_ex, seq, d_ff = u.shape
+    d_model = x.shape[-1]
+    pairs = n_ex // 2
+    per_grad = 2 * pairs
+    per_step = per_grad // 4
+    n_grads = 2 * n_layers
+    steps = n_grads * per_grad
+    last = n_layers - 2
     pos = place()
     core, partner = pos[0], pos[5]
-    enter(pos[3:])
+    ring = Ring(size, sums, got_z, z_sems, grads)
+    barrier = pltpu.get_barrier_semaphore()
+    for peer in pos[3:]:
+        pl.semaphore_signal(barrier, inc=1, device_id={"tp": peer}, device_id_type=pl.DeviceIdType.MESH)
+    if size > 1:
+        for peer in ring.peers:
+            pl.semaphore_signal(barrier, inc=1, device_id={"dp": peer}, device_id_type=pl.DeviceIdType.MESH)
+    pl.semaphore_wait(barrier, 5 if size > 1 else 3)
     ex = Exchange(pos, part, cot, got1, got2, sems, n_ex, n_ex)
 
     def in_copies(e):
         return [
             pltpu.make_async_copy(part_in.at[e], part.at[e], in_sems.at[e, 0]),
-            pltpu.make_async_copy(cot_in.at[core, e], cot.at[e], in_sems.at[e, 1]),
+            pltpu.make_async_copy(dx_in.at[last, core, e], cot.at[e], in_sems.at[e, 1]),
         ]
 
     def dx_copies(j):
         s = lax.rem(j, 4)
-        near = pltpu.make_async_copy(cot.at[j], dx_out.at[core, j], dx_sems.at[s, 0])
-        far = push(cot.at[j], dx_out.at[core, j], dx_sems.at[s, 1], all_sems.at[0], partner)
+        near = pltpu.make_async_copy(cot.at[j], d_in.at[core, j], dx_sems.at[s, 0])
+        far = push(cot.at[j], d_in.at[core, j], dx_sems.at[s, 1], all_sems.at[0], partner)
         return near, far
 
     def save(j):
@@ -375,47 +453,140 @@
         near.wait()
         far.wait_send()
 
+    def where_is(t):
+        g, pair = lax.div(t, per_grad), lax.rem(t, per_grad)
+        return g, lax.rem(g, n_layers), lax.div(pair, pairs), 2 * lax.rem(pair, pairs), lax.rem(t, 2)
+
+    def load(t):
+        g, layer, m, e, s = where_is(t)
+        two = pl.ds(e, 2)
+
+        @pl.when(g < n_layers)
+        def _():
+            pltpu.make_async_copy(x.at[layer, m, two], a_buf.at[s], load_sems.at[s, 0]).start()
+            pltpu.make_async_copy(dh.at[layer, m, two], b_buf.at[s], load_sems.at[s, 1]).start()
+
+        @pl.when(g >= n_layers)
+        def _():
+            pltpu.make_async_copy(u.at[layer, m, two], b_buf.at[s], load_sems.at[s, 1]).start()
+
+        @pl.when(g == n_grads - 1)
+        def _():
+            pltpu.make_async_copy(d_out.at[m, two], a_buf.at[s], load_sems.at[s, 0]).start()
+
+        @pl.when(jnp.logical_and(g >= n_layers, g < n_grads - 1))
+        def _():
+            pltpu.make_async_copy(dx_in.at[last - layer, m, two], a_buf.at[s], load_sems.at[s, 0]).start()
+
+    def accumulate(t):
+        g, layer, m, e, s = where_is(t)
+
+        @pl.when(t + 1 < steps)
+        def _():
+            load(t + 1)
+
+        pltpu.make_async_copy(x.at[0, 0, pl.ds(0, 2)], a_buf.at[s], load_sems.at[s, 0]).wait()
+        pltpu.make_async_copy(u.at[0, 0, pl.ds(0, 2)], b_buf.at[s], load_sems.at[s, 1]).wait()
+        slot = lax.rem(g, 3)
+
+        def add(b, a):
+            c = lax.dot_general(b, a, (((0,), (0,)), ((), ())), preferred_element_type=F32)
+            tiles, _, rows, columns = sums.shape[1:]
+            first = lax.rem(t, per_grad) == 0
+            for n in range(2 * size):
+                new = c[:, n * columns:(n + 1) * columns].reshape(tiles, rows, columns)
+                old = jnp.where(first, 0.0, sums[slot, :, n])
+                sums[slot, :, n] = old + new
+
+        @pl.when(g < n_layers)
+        def _():
+            for i in range(2):
+                b_scaled[i * seq:(i + 1) * seq] = (b_buf[s, i].astype(F32) * clip[m * n_ex + e + i]).astype(BF16)
+            add(b_scaled[...], a_buf[s].reshape(2 * seq, d_model))
+
+        @pl.when(g >= n_layers)
+        def _():
+            for i in range(2):
+                a_scaled[i * seq:(i + 1) * seq] = (a_buf[s, i].reshape(seq, d_model).astype(F32) * clip[m * n_ex + e + i]).astype(BF16)
+                b_scaled[i * seq:(i + 1) * seq] = gelu(b_buf[s, i].astype(F32)).astype(BF16)
+            add(b_scaled[...], a_scaled[...])
+
+    load(0)
+
     @pl.loop(0, n_ex)
     def _(e):
         for copy in in_copies(e):
             copy.start()
 
-    @pl.loop(0, n_ex + 5 * LAG)
-    def _(k):
-        run_stages(ex, k, n_ex, save, saved)
-
-        @pl.when(k < n_ex)
-        def _():
-            for copy in in_copies(k):
-                copy.wait()
-            ex.start(0, k)
-
-    pltpu.make_async_copy(dx_out.at[1 - core], dx_out.at[1 - core], all_sems.at[0]).wait()
-
-
-def sum_call(part, cot):
-    n_ex = part.shape[0]
+    blocks = 4 * n_grads
+
+    @pl.loop(0, max(blocks + 4 + size - 1, 2 * (n_ex + 5 * LAG)))
+    def _(i):
+        j = i - 4
+        for step in reversed(range(size)):
+            @pl.when(jnp.logical_and(j - step >= 0, j - step < blocks))
+            def _(step=step):
+                if step == 0:
+                    ring.start(0, j)
+                else:
+                    ring.add(step - 1, j - step)
+
+        @pl.when(lax.rem(i, 2) == 0)
+        def _():
+            k = lax.div(i, 2)
+
+            @pl.when(k < n_ex)
+            def _():
+                for copy in in_copies(k):
+                    copy.wait()
+                ex.start(0, k)
+
+            run_stages(ex, k, n_ex, save, saved)
+
+        @pl.when(i < blocks)
+        def _():
+            @pl.loop(0, per_step)
+            def _(r):
+                accumulate(i * per_step + r)
+
+    pltpu.make_async_copy(d_in.at[1 - core], d_in.at[1 - core], all_sems.at[0]).wait()
+
+
+def gradient_call(size, part, dx, d_out, x, dh, u, clip):
+    n_layers, _, n_ex, seq, d_ff = u.shape
+    d_model = x.shape[-1]
     pieces = part.shape[1:]
+    width = d_model // (2 * size)
     dma = pltpu.SemaphoreType.DMA
     return pl.pallas_call(
-        sum_kernel,
-        out_shape=jax.ShapeDtypeStruct((2, n_ex) + pieces, BF16),
-        in_specs=[ANY] * 2,
-        out_specs=ANY,
+        functools.partial(gradient_kernel, size),
+        out_shape=(
+            jax.ShapeDtypeStruct((2, n_ex) + pieces, BF16),
+            jax.ShapeDtypeStruct((2 * n_layers, d_ff, 2 * width), F32),
+        ),
+        in_specs=[ANY] * 6 + [pl.BlockSpec(memory_space=pltpu.SMEM)],
+        out_specs=(ANY, VMEM),
         scratch_shapes=[
             pltpu.VMEM((n_ex,) + pieces, BF16),
             pltpu.VMEM((n_ex,) + pieces, BF16),
             pltpu.VMEM((4, 2, 2) + pieces[1:], BF16),
             pltpu.VMEM((4, 2) + pieces[1:], BF16),
+            pltpu.VMEM((3, 4, 2 * size, d_ff // 4, width), F32),
+            pltpu.VMEM((size - 1, 4, 2, d_ff // 4, width), F32),
+            pltpu.VMEM((2, 2) + pieces, BF16),
+            pltpu.VMEM((2, 2, seq, d_ff), BF16),
+            pltpu.VMEM((2 * seq, d_model), BF16),
+            pltpu.VMEM((2 * seq, d_ff), BF16),
             dma((2, 4, 4, 2)),
             dma((n_ex, 2)),
             dma((4, 2)),
             dma((1,)),
+            dma((2, size - 1, 4, 2)),
+            dma((2, 2)),
         ],
-        compiler_params=pltpu.CompilerParams(collective_id=1, has_side_effects=True, vmem_limit_bytes=40_000_000),
-        cost_estimate=pl.CostEstimate(flops=200_000_000_000, bytes_accessed=part.size * 8, transcendentals=0),
-        name="sum_rows",
-    )(part, cot)
+        compiler_params=pltpu.CompilerParams(collective_id=1, has_side_effects=True, vmem_limit_bytes=66_000_000),
+        name="gradient",
+    )(part, dx, d_out.reshape((2, n_ex) + pieces), x.reshape((n_layers, 2, n_ex) + pieces), dh, u, clip)
 
 
 def solution(mesh):
@@ -429,28 +600,14 @@
         own_norm = jnp.sum(norms, axis=(1, 2))
         norm_part = jnp.where(jnp.arange(2)[:, None] == core, own_norm[None, :], 0.0)
         norm_vec = lax.psum(norm_part, "tp")
-        clip_col = jnp.minimum(1.0, clip_norm[0] / jnp.sqrt(norm_vec))[:, :, None, None]
+        clip_fac = jnp.minimum(1.0, clip_norm[0] / jnp.sqrt(norm_vec)).reshape(-1)
         noise_scale = noise_mult[0] * clip_norm[0]
-        up_parts, down_parts = [], []
-        for layer_idx in range(n_layers):
-            if layer_idx == n_layers - 1:
-                cot_layer = d_out
-            else:
-                cot_layer = dx[n_layers - 2 - layer_idx].reshape(d_out.shape)
-            hidden = jax.nn.gelu(u_pre[layer_idx].astype(F32)).astype(BF16)
-            scaled_dh = (dh[layer_idx] * clip_col).astype(BF16)
-            scaled_cot = (cot_layer * clip_col).astype(BF16)
-            up_parts.append(jnp.einsum("mbtd,mbtn->dn", x_in[layer_idx], scaled_dh, preferred_element_type=F32))
-            down_parts.append(jnp.einsum("mbtn,mbtd->nd", hidden, scaled_cot, preferred_element_type=F32))
-        late_part, _ = lax.optimization_barrier((part, (up_parts, down_parts)))
-        d_in = sum_call(late_part, dx[n_layers - 2]).reshape(d_out.shape)
-        up_grads, down_grads = [], []
-        for layer_idx in range(n_layers):
-            up_sum = lax.psum_scatter(up_parts[layer_idx], "dp", scatter_dimension=0, tiled=True)
-            down_sum = lax.psum_scatter(down_parts[layer_idx], "dp", scatter_dimension=1, tiled=True)
-            up_grads.append((up_sum + noise_scale * noise_up[layer_idx]) / examples)
-            down_grads.append((down_sum + noise_scale * noise_down[layer_idx]) / examples)
-        return jnp.stack(up_grads), jnp.stack(down_grads), d_in
+        d_in, sums = gradient_call(dp_size, part, dx, d_out, x_in, dh, u_pre, clip_fac)
+        up_sum = jnp.swapaxes(sums[:n_layers], 1, 2)
+        down_sum = sums[n_layers:]
+        up_grad = (up_sum + noise_scale * noise_up) / examples
+        down_grad = (down_sum + noise_scale * noise_down) / examples
+        return up_grad, down_grad, d_in.reshape(d_out.shape)
 
     in_specs = (P(None, None, "dp", None, None), P(None, None, "dp", None, "tp"), P(None, None, "tp"), P(None, "tp", None), P(None, "dp", None, None), P(None, "dp", "tp"), P(None, "tp", "dp"), P(), P())
     out_specs = (P(None, "dp", "tp"), P(None, "tp", "dp"), P(None, "dp", None, None))

time: 849 us -> 624 us (0.73)
  matrix products: 105 us -> 0 us
  other arithmetic: 100 us -> 5.54 us
  local copies, waits for them, and re-layouts: 93.9 us -> 20.7 us
  Pallas kernels: 521 us -> 583 us
  between operations: 15.5 us -> 1.99 us
    dot_general x6 -> x0, matrix products: 105 us -> none  [the longest x3 52.6 us: local_pass(): jnp.einsum('mbtd,mbtn->dn', x_in[layer_idx], scaled_dh, preferred_element...]
    convert_element_type x3 -> x0, other arithmetic: 92.2 us -> none  [the longest x1 47.7 us: local_pass(): scaled_cot = (cot_layer * clip_col).astype(BF16)]
    pallas_call x1, Pallas kernels: 158 us -> 240 us  [gradient_call(): pl.pallas_call(functools.partial(gradient_kernel, size), out_shape=(jax.S...]
    slice x2 -> x0, local copies, waits for them, and re-layouts: 40.3 us -> none  [the longest x1 40.1 us: local_pass(): x_in[layer_idx]]
    squeeze x1 -> x0, local copies, waits for them, and re-layouts: 31.1 us -> none  [local_pass(): d_in = sum_call(late_part, dx[n_layers - 2]).reshape(d_out.shape)]
    pallas_call x1, Pallas kernels: 363 us -> 342 us  [backward_call(): pl.pallas_call(backward_kernel, out_shape=(jax.ShapeDtypeStruct((n_layers...]
    unnamed x9 -> x5, local copies, waits for them, and re-layouts: 22.5 us -> 20.1 us
  transfers between devices with their start and end apart: 6 -> 0, of which waited for: 0 -> 0; matrix products, arithmetic and copies ran while one was open for 23% -> 0% of each run, Pallas kernels for 19% -> 0%
where the time goes in v2:
time: 624 us; the launch traced here: 623 us
  Pallas kernels  583 us (93%)
  local copies, waits for them, and re-layouts  20.7 us (3%)
  blocking collectives  11.8 us (2%)
    pallas_call x1, Pallas kernels, backward_call(): pl.pallas_call(backward_kernel, out_shape=(jax.ShapeDtypeStruct((n_layers...  342 us
    pallas_call x1, Pallas kernels, gradient_call(): pl.pallas_call(functools.partial(gradient_kernel, size), out_shape=(jax.S...  240 us
    unnamed x5, local copies, waits for them, and re-layouts  20.1 us

profile of v2, /device:TPU:0, one launch (start us, length us, event | category | flops | bytes accessed | tf_op | source)
XLA Modules:
  0.0 622.6 jit_solution(5331394407272636100)
XLA Ops:
  0.6 342.2 %backward.1 = (bf16[2,2,12,8,48,1024]{5,4,3,2,1,0:T(8,128)(2,1)}, bf16[3,2,12,384,512]{4,3,2,1,0:T(8,128)(2,1)}, bf16[12,8,48,1024]{3,2,1,0:T(8,128)(2,1)}, f32[12,8,384]{2,1,0:T(8,128)}) custom-call(bf16[3,2,12,384,512]{4,3,2,1,0:T(8,128)(2,1)} %u.3, bf16[3,2,12,384,1024]{4,3,2,1,0:T(8,128)(2,1)} %x.1, bf16[3,1024,512]{2,1,0:T(8,128)(2,1)} %w_up.1, ...), custom_call_target="tpu_custom_call" | custom-call | flops 115964116992 | bytes 226492416 | tf_op jit(solution)/shard_map/backward/pallas_call | solution.py:322
  342.9 1.1 reduce_sum.9
  343.9 0.1 broadcast_select_fusion
  344.0 11.8 %psum.7 = f32[2,12]{1,0:T(2,128)S(1)} all-reduce(f32[2,12]{1,0:T(2,128)S(1)} %broadcast_select_fusion), channel_id=1, replica_groups=mesh['dp'=4,'tp'=8] {'tp'}, use_global_device_ids=true, to_apply=%region_1.2 | all-reduce | flops 24 | bytes 192 | tf_op jit(solution)/shard_map/psum | solution.py:602
  356.5 0.6 reshape.27.clip
  357.1 240.4 %gradient.1 = (bf16[2,12,8,48,1024]{4,3,2,1,0:T(8,128)(2,1)}, f32[6,512,256]{2,1,0:T(8,128)}) custom-call(bf16[12,8,48,1024]{3,2,1,0:T(8,128)(2,1)} %get-tuple-element.9.part_in, bf16[2,2,12,8,48,1024]{5,4,3,2,1,0:T(8,128)(2,1)} %get-tuple-element.10.dx_in, bf16[2,12,8,48,1024]{4,3,2,1,0:T(8,128)(2,1)} %bitcast.15, ...), custom_call_target="tpu_custom_call" | custom-call | tf_op jit(solution)/shard_map/gradient/pallas_call | solution.py:561
  598.1 1.9 copy.12
  600.0 1.6 fusion
  601.6 0.0 copy-start
  601.6 1.6 copy.13
  603.3 0.0 copy-done
  603.3 2.8 add_multiply_fusion
  606.0 16.6 %copy.17 = bf16[2,12,384,1024]{3,2,1,0:T(8,128)(2,1)} copy(bf16[2,12,384,1024]{3,2,1,0:T(8,128)(2,1)} %bitcast.13) | data formatting | bytes 37748736
  (2 shorter events, 0.0 us)
Async XLA Ops:
  601.6 1.6 copy-start

commit v3 on v2

--- a/solution.py
+++ b/solution.py
@@ -14,7 +14,7 @@
 ANY = pl.BlockSpec(memory_space=pl.ANY)
 VMEM = pl.BlockSpec(memory_space=pltpu.VMEM)
 LAG = 1
-U_GROUP = 4
+U_GROUP = 2
 COEF = math.sqrt(2.0 / math.pi)
 CUBE = 0.044715
 
@@ -111,7 +111,7 @@
     at(1, ex.add_first)
 
 
-def backward_kernel(u, x, w_up, w_down, d_out, dx_out, dh_out, part_out, norm_out, cot, w1, w2, u_own, u_far, x_buf, d_act, hid, dh, part, got1, got2, gram_a, gram_b, sems, w_sems, u_sems, cot_sems, load_sems, dh_sems, dx_sems, all_sems, part_sems):
+def backward_kernel(u, x, w_up, w_down, d_out, dx_out, dh_out, part_out, norm_out, norm_acc, norm_own, norm_all, norm_sems, cot, w1, w2, u_own, u_far, x_buf, d_act, hid, dh, part, got1, got2, gram_a, gram_b, sems, w_sems, u_sems, cot_sems, load_sems, dh_sems, dx_sems, all_sems, part_sems):
     n_layers, _, n_ex, seq, d_ff = u.shape
     d_model = x.shape[-1]
     pieces = cot.shape[1:]
@@ -120,7 +120,9 @@
     summed = total - n_ex
     pos = place()
     core, partner = pos[0], pos[5]
-    enter(pos[3:])
+    me = lax.axis_index("tp")
+    others = [lax.rem(me + d, 8) for d in range(1, 8)]
+    enter(others)
     ex = Exchange(pos, part, cot, got1, got2, sems, n_ex, 4)
 
     def layer_of(k):
@@ -213,7 +215,8 @@
     def _(g):
         far_copy(g).start()
 
-    norm_out[...] = jnp.zeros_like(norm_out)
+    norm_acc[...] = jnp.zeros_like(norm_acc)
+    norm_own[...] = jnp.zeros_like(norm_own)
 
     def compute(p):
         k, s = example_at(p), lax.rem(p, 2)
@@ -285,7 +288,7 @@
         for left, right in ((hid[...], cot[e].reshape(seq, d_model)), (x_buf[s], dh[s])):
             gram_a[...] = lax.dot_general(left, left, NT, preferred_element_type=F32)
             gram_b[...] = lax.dot_general(right, right, NT, preferred_element_type=F32)
-            norm_out[e] += jnp.sum((gram_a[...] * gram_b[...]).reshape(seq // 8, 8, seq), axis=0)
+            norm_acc[e] += jnp.sum((gram_a[...] * gram_b[...]).reshape(seq // 8, 8, seq), axis=0)
 
     @pl.loop(0, summed + 5 * LAG)
     def _(i):
@@ -294,6 +297,11 @@
         @pl.loop(first_of(i), first_of(i + 1))
         def _(p):
             compute(p)
+
+    norm_own[0:n_ex] = jnp.sum(norm_acc[...], axis=1)
+    for peer in others:
+        push(norm_own, norm_all.at[me], norm_sems.at[0, peer], norm_sems.at[1, me], peer).start()
+    norm_all[me] = norm_own[...]
 
     for k in (total - 2, total - 1):
         part_copy(k).wait()
@@ -301,6 +309,10 @@
         near, far = dh_copies(k)
         near.wait()
         far.wait_send()
+    for peer in others:
+        push(norm_own, norm_all.at[peer], norm_sems.at[0, peer], norm_sems.at[1, peer], peer).wait()
+    for m in range(2):
+        norm_out[m] = norm_all[m] + norm_all[m + 2] + norm_all[m + 4] + norm_all[m + 6]
     pltpu.make_async_copy(dh_out.at[:, 1 - core], dh_out.at[:, 1 - core], all_sems.at[0]).wait()
     pltpu.make_async_copy(dx_out.at[:, 1 - core], dx_out.at[:, 1 - core], all_sems.at[1]).wait()
     for layer in range(n_layers):
@@ -325,11 +337,15 @@
             jax.ShapeDtypeStruct((n_layers - 1, 2, n_ex) + pieces, BF16),
             jax.ShapeDtypeStruct((n_layers, 2, n_ex, seq, d_ff), BF16),
             jax.ShapeDtypeStruct((n_ex,) + pieces, BF16),
-            jax.ShapeDtypeStruct((n_ex, 8, seq), F32),
+            jax.ShapeDtypeStruct((2, 16, seq), F32),
         ),
         in_specs=[ANY] * 5,
         out_specs=(ANY, ANY, ANY, VMEM),
         scratch_shapes=[
+            pltpu.VMEM((n_ex, 8, seq), F32),
+            pltpu.VMEM((16, seq), F32),
+            pltpu.VMEM((8, 16, seq), F32),
+            dma((2, 8)),
             pltpu.VMEM((n_ex,) + pieces, BF16),
             pltpu.VMEM((n_layers, d_model, 2 * d_ff), BF16),
             pltpu.VMEM((n_layers, 2 * d_ff, d_model), BF16),
@@ -523,7 +539,7 @@
     @pl.loop(0, max(blocks + 4 + size - 1, 2 * (n_ex + 5 * LAG)))
     def _(i):
         j = i - 4
-        for step in reversed(range(size)):
+        for step in (0, *reversed(range(1, size))):
             @pl.when(jnp.logical_and(j - step >= 0, j - step < blocks))
             def _(step=step):
                 if step == 0:
@@ -589,24 +605,73 @@
     )(part, dx, d_out.reshape((2, n_ex) + pieces), x.reshape((n_layers, 2, n_ex) + pieces), dh, u, clip)
 
 
+def finish_kernel(examples, n_layers, d_in, up_sum, down_sum, noise_up, noise_down, clip_norm, noise_mult, up_grad, down_grad, d_in_out):
+    i = pl.program_id(0)
+    d_in_out[...] = d_in[...]
+    noise_scale = noise_mult[0] * clip_norm[0]
+
+    @pl.when(i < n_layers)
+    def _():
+        up_grad[0] = (up_sum[0].T + noise_scale * noise_up[0]) / examples
+
+    @pl.when(i >= n_layers)
+    def _():
+        down_grad[0] = (down_sum[0] + noise_scale * noise_down[0]) / examples
+
+
+def finish_call(examples, d_in, sums, noise_up, noise_down, clip_norm, noise_mult):
+    n_layers, width, d_ff = noise_up.shape
+    rows, seq, d_model = d_in.shape
+    steps = 2 * n_layers
+
+    def early(i):
+        return jnp.minimum(i, n_layers - 1), 0, 0
+
+    def late(i):
+        return jnp.maximum(i - n_layers, 0), 0, 0
+
+    def late_sum(i):
+        return jnp.maximum(i, n_layers), 0, 0
+
+    def same(i):
+        return i, 0, 0
+
+    smem = pl.BlockSpec(memory_space=pltpu.SMEM)
+    block = pl.BlockSpec((rows // steps, seq, d_model), same)
+    return pl.pallas_call(
+        functools.partial(finish_kernel, examples, n_layers),
+        grid=(steps,),
+        out_shape=(
+            jax.ShapeDtypeStruct((n_layers, width, d_ff), F32),
+            jax.ShapeDtypeStruct((n_layers, d_ff, width), F32),
+            jax.ShapeDtypeStruct(d_in.shape, BF16),
+        ),
+        in_specs=[
+            block,
+            pl.BlockSpec((1, d_ff, width), early),
+            pl.BlockSpec((1, d_ff, width), late_sum),
+            pl.BlockSpec((1, width, d_ff), early),
+            pl.BlockSpec((1, d_ff, width), late),
+            smem,
+            smem,
+        ],
+        out_specs=(pl.BlockSpec((1, width, d_ff), early), pl.BlockSpec((1, d_ff, width), late), block),
+        compiler_params=pltpu.CompilerParams(vmem_limit_bytes=66_000_000),
+        name="finish",
+    )(d_in, sums, sums, noise_up, noise_down, clip_norm, noise_mult)
+
+
 def solution(mesh):
     dp_size = mesh.shape["dp"]
 
     def local_pass(x_in, u_pre, w_up, w_down, d_out, noise_up, noise_down, clip_norm, noise_mult):
-        n_layers = x_in.shape[0]
         examples = d_out.shape[0] * d_out.shape[1] * dp_size
-        core = lax.rem(lax.axis_index("tp"), 2)
         dx, dh, part, norms = backward_call(u_pre, x_in, w_up, w_down, d_out)
-        own_norm = jnp.sum(norms, axis=(1, 2))
-        norm_part = jnp.where(jnp.arange(2)[:, None] == core, own_norm[None, :], 0.0)
-        norm_vec = lax.psum(norm_part, "tp")
+        norm_vec = jnp.sum(norms, axis=2)[:, :d_out.shape[1]]
         clip_fac = jnp.minimum(1.0, clip_norm[0] / jnp.sqrt(norm_vec)).reshape(-1)
-        noise_scale = noise_mult[0] * clip_norm[0]
         d_in, sums = gradient_call(dp_size, part, dx, d_out, x_in, dh, u_pre, clip_fac)
-        up_sum = jnp.swapaxes(sums[:n_layers], 1, 2)
-        down_sum = sums[n_layers:]
-        up_grad = (up_sum + noise_scale * noise_up) / examples
-        down_grad = (down_sum + noise_scale * noise_down) / examples
+        d_in = d_in.reshape((-1,) + d_out.shape[2:])
+        up_grad, down_grad, d_in = finish_call(examples, d_in, sums, noise_up, noise_down, clip_norm, noise_mult)
         return up_grad, down_grad, d_in.reshape(d_out.shape)
 
     in_specs = (P(None, None, "dp", None, None), P(None, None, "dp", None, "tp"), P(None, None, "tp"), P(None, "tp", None), P(None, "dp", None, None), P(None, "dp", "tp"), P(None, "tp", "dp"), P(), P())

time: 624 us -> 608 us (0.974)
  local copies, waits for them, and re-layouts: 20.7 us -> 0.59 us
  Pallas kernels: 583 us -> 602 us
  blocking collectives: 11.8 us -> 0 us
    unnamed x5 -> x0, local copies, waits for them, and re-layouts: 20.1 us -> none
    pallas_call x0 -> x1, Pallas kernels: none -> 16.4 us  [finish_call(): pl.pallas_call(functools.partial(finish_kernel, examples, n_layers), grid...]
    psum x1 -> x0, blocking collectives: 11.8 us -> none  [local_pass(): norm_vec = lax.psum(norm_part, 'tp')]
where the time goes in v3:
time: 608 us; the launch traced here: 606 us
  Pallas kernels  602 us (99%)
    pallas_call x1, Pallas kernels, backward_call(): pl.pallas_call(backward_kernel, out_shape=(jax.ShapeDtypeStruct((n_layers...  345 us
    pallas_call x1, Pallas kernels, gradient_call(): pl.pallas_call(functools.partial(gradient_kernel, size), out_shape=(jax.S...  240 us
    pallas_call x1, Pallas kernels, finish_call(): pl.pallas_call(functools.partial(finish_kernel, examples, n_layers), grid...  16.4 us

profile of v3, /device:TPU:0, one launch (start us, length us, event | category | flops | bytes accessed | tf_op | source)
XLA Modules:
  0.0 605.6 jit_solution(16481920519482294257)
XLA Ops:
  0.6 345.3 %backward.1 = (bf16[2,2,12,8,48,1024]{5,4,3,2,1,0:T(8,128)(2,1)}, bf16[3,2,12,384,512]{4,3,2,1,0:T(8,128)(2,1)}, bf16[12,8,48,1024]{3,2,1,0:T(8,128)(2,1)}, f32[2,16,384]{2,1,0:T(8,128)}) custom-call(bf16[3,2,12,384,512]{4,3,2,1,0:T(8,128)(2,1)} %u.3, bf16[3,2,12,384,1024]{4,3,2,1,0:T(8,128)(2,1)} %x.1, bf16[3,1024,512]{2,1,0:T(8,128)(2,1)} %w_up.1, ...), custom_call_target="tpu_custom_call" | custom-call | flops 115964116992 | bytes 226492416 | tf_op jit(solution)/shard_map/backward/pallas_call | solution.py:334
  345.9 0.9 reduce_sum.9
  347.5 0.6 reshape.24.clip
  348.1 240.4 %gradient.1 = (bf16[2,12,8,48,1024]{4,3,2,1,0:T(8,128)(2,1)}, f32[6,512,256]{2,1,0:T(8,128)}) custom-call(bf16[12,8,48,1024]{3,2,1,0:T(8,128)(2,1)} %get-tuple-element.12.part_in, bf16[2,2,12,8,48,1024]{5,4,3,2,1,0:T(8,128)(2,1)} %get-tuple-element.13.dx_in, bf16[2,12,8,48,1024]{4,3,2,1,0:T(8,128)(2,1)} %bitcast.9, ...), custom_call_target="tpu_custom_call" | custom-call | tf_op jit(solution)/shard_map/gradient/pallas_call | solution.py:577
  589.1 16.4 %finish.1 = (f32[3,256,512]{2,1,0:T(8,128)}, f32[3,512,256]{2,1,0:T(8,128)}, bf16[24,384,1024]{2,1,0:T(8,128)(2,1)}) custom-call(bf16[24,384,1024]{2,1,0:T(8,128)(2,1)} %bitcast.7, f32[6,512,256]{2,1,0:T(8,128)} %get-tuple-element.17.up_sum.down_sum, f32[6,512,256]{2,1,0:T(8,128)} %get-tuple-element.17.up_sum.down_sum, f32[3,256,512]{2,1,0:T(8,128)} %noise_up.1, ...), custom_call_target="tpu_custom_call" | custom-call | tf_op jit(solution)/shard_map/finish/pallas_call | solution.py:641
  (1 shorter events, 0.0 us)

commit v4 on v3

--- a/solution.py
+++ b/solution.py
@@ -393,8 +393,8 @@
         return 2 * lax.rem(self.z + 1 + step, self.size) + 1
 
     def copies(self, step, j):
-        s = lax.rem(j, 4)
-        block = self.sums.at[lax.rem(lax.div(j, 4), 3), lax.rem(j, 4)]
+        s = lax.rem(j, 8)
+        block = self.sums.at[lax.rem(lax.div(j, 4), 4), lax.rem(j, 4)]
         return [
             pltpu.make_async_remote_copy(
                 src_ref=block.at[self.tile(step, way)],
@@ -414,9 +414,9 @@
     def add(self, step, j):
         for copy in self.copies(step, j):
             copy.wait()
-        g, q, s = lax.div(j, 4), lax.rem(j, 4), lax.rem(j, 4)
+        g, q, s = lax.div(j, 4), lax.rem(j, 4), lax.rem(j, 8)
         for way in range(2):
-            at = lax.rem(g, 3), q, self.tile(step + 1, way)
+            at = lax.rem(g, 4), q, self.tile(step + 1, way)
             total = self.sums[at] + self.got[step, s, way]
             if step + 1 < self.size - 1:
                 self.sums[at] = total
@@ -503,7 +503,7 @@
 
         pltpu.make_async_copy(x.at[0, 0, pl.ds(0, 2)], a_buf.at[s], load_sems.at[s, 0]).wait()
         pltpu.make_async_copy(u.at[0, 0, pl.ds(0, 2)], b_buf.at[s], load_sems.at[s, 1]).wait()
-        slot = lax.rem(g, 3)
+        slot = lax.rem(g, 4)
 
         def add(b, a):
             c = lax.dot_general(b, a, (((0,), (0,)), ((), ())), preferred_element_type=F32)
@@ -536,16 +536,16 @@
 
     blocks = 4 * n_grads
 
-    @pl.loop(0, max(blocks + 4 + size - 1, 2 * (n_ex + 5 * LAG)))
+    @pl.loop(0, max(blocks + 4 + 2 * (size - 1), 2 * (n_ex + 5 * LAG)))
     def _(i):
         j = i - 4
         for step in (0, *reversed(range(1, size))):
-            @pl.when(jnp.logical_and(j - step >= 0, j - step < blocks))
+            @pl.when(jnp.logical_and(j - 2 * step >= 0, j - 2 * step < blocks))
             def _(step=step):
                 if step == 0:
                     ring.start(0, j)
                 else:
-                    ring.add(step - 1, j - step)
+                    ring.add(step - 1, j - 2 * step)
 
         @pl.when(lax.rem(i, 2) == 0)
         def _():
@@ -587,8 +587,8 @@
             pltpu.VMEM((n_ex,) + pieces, BF16),
             pltpu.VMEM((4, 2, 2) + pieces[1:], BF16),
             pltpu.VMEM((4, 2) + pieces[1:], BF16),
-            pltpu.VMEM((3, 4, 2 * size, d_ff // 4, width), F32),
-            pltpu.VMEM((size - 1, 4, 2, d_ff // 4, width), F32),
+            pltpu.VMEM((4, 4, 2 * size, d_ff // 4, width), F32),
+            pltpu.VMEM((size - 1, 8, 2, d_ff // 4, width), F32),
             pltpu.VMEM((2, 2) + pieces, BF16),
             pltpu.VMEM((2, 2, seq, d_ff), BF16),
             pltpu.VMEM((2 * seq, d_model), BF16),
@@ -597,7 +597,7 @@
             dma((n_ex, 2)),
             dma((4, 2)),
             dma((1,)),
-            dma((2, size - 1, 4, 2)),
+            dma((2, size - 1, 8, 2)),
             dma((2, 2)),
         ],
         compiler_params=pltpu.CompilerParams(collective_id=1, has_side_effects=True, vmem_limit_bytes=66_000_000),

time: 608 us -> 605 us (level)
  no operation moved by 1% of the time
where the time goes in v4:
time: 605 us; the launch traced here: 604 us
  Pallas kernels  600 us (99%)
    pallas_call x1, Pallas kernels, backward_call(): pl.pallas_call(backward_kernel, out_shape=(jax.ShapeDtypeStruct((n_layers...  345 us
    pallas_call x1, Pallas kernels, gradient_call(): pl.pallas_call(functools.partial(gradient_kernel, size), out_shape=(jax.S...  239 us
    pallas_call x1, Pallas kernels, finish_call(): pl.pallas_call(functools.partial(finish_kernel, examples, n_layers), grid...  16.4 us

profile of v4, /device:TPU:0, one launch (start us, length us, event | category | flops | bytes accessed | tf_op | source)
XLA Modules:
  0.0 603.8 jit_solution(11762698032078072000)
XLA Ops:
  0.6 345.3 %backward.1 = (bf16[2,2,12,8,48,1024]{5,4,3,2,1,0:T(8,128)(2,1)}, bf16[3,2,12,384,512]{4,3,2,1,0:T(8,128)(2,1)}, bf16[12,8,48,1024]{3,2,1,0:T(8,128)(2,1)}, f32[2,16,384]{2,1,0:T(8,128)}) custom-call(bf16[3,2,12,384,512]{4,3,2,1,0:T(8,128)(2,1)} %u.3, bf16[3,2,12,384,1024]{4,3,2,1,0:T(8,128)(2,1)} %x.1, bf16[3,1024,512]{2,1,0:T(8,128)(2,1)} %w_up.1, ...), custom_call_target="tpu_custom_call" | custom-call | flops 115964116992 | bytes 226492416 | tf_op jit(solution)/shard_map/backward/pallas_call | solution.py:334
  345.9 0.9 reduce_sum.9
  347.5 0.6 reshape.24.clip
  348.1 238.6 %gradient.1 = (bf16[2,12,8,48,1024]{4,3,2,1,0:T(8,128)(2,1)}, f32[6,512,256]{2,1,0:T(8,128)}) custom-call(bf16[12,8,48,1024]{3,2,1,0:T(8,128)(2,1)} %get-tuple-element.12.part_in, bf16[2,2,12,8,48,1024]{5,4,3,2,1,0:T(8,128)(2,1)} %get-tuple-element.13.dx_in, bf16[2,12,8,48,1024]{4,3,2,1,0:T(8,128)(2,1)} %bitcast.9, ...), custom_call_target="tpu_custom_call" | custom-call | tf_op jit(solution)/shard_map/gradient/pallas_call | solution.py:577
  587.3 16.4 %finish.1 = (f32[3,256,512]{2,1,0:T(8,128)}, f32[3,512,256]{2,1,0:T(8,128)}, bf16[24,384,1024]{2,1,0:T(8,128)(2,1)}) custom-call(bf16[24,384,1024]{2,1,0:T(8,128)(2,1)} %bitcast.7, f32[6,512,256]{2,1,0:T(8,128)} %get-tuple-element.17.up_sum.down_sum, f32[6,512,256]{2,1,0:T(8,128)} %get-tuple-element.17.up_sum.down_sum, f32[3,256,512]{2,1,0:T(8,128)} %noise_up.1, ...), custom_call_target="tpu_custom_call" | custom-call | tf_op jit(solution)/shard_map/finish/pallas_call | solution.py:641
  (1 shorter events, 0.0 us)
